TPU v7x, 8 devices: a whole 2x2x1 slice. The times are simulated.
8 devices in a mesh: dp: 1 (over z), tp: 8 (over y, x, core).
Axes of the slice: x: 2, y: 2, z: 1, core: 2. Of those that a mesh axis runs over, the one named last changes fastest.
Arguments:
- tokens: bfloat16 [8, 2048, 1536], P('dp', 'tp')
- pad_mask: int32 [8, 2048], P('dp')
- rel_table: float32 [32, 16], P(None, 'tp')
- w_query: bfloat16 [2, 1536, 1024], P(None, None, 'tp')
- w_key: bfloat16 [2, 1536, 1024], P(None, None, 'tp')
- w_value: bfloat16 [2, 1536, 1024], P(None, None, 'tp')
- w_out: bfloat16 [2, 1024, 1536], P(None, 'tp')
- w_act: bfloat16 [2, 1536, 3840], P(None, None, 'tp')
- w_lin: bfloat16 [2, 1536, 3840], P(None, None, 'tp')
- w_down: bfloat16 [2, 3840, 1536], P(None, 'tp')
- norm_attn: float32 [2, 1536], replicated
- norm_mlp: float32 [2, 1536], replicated
Outputs:
- output: bfloat16 [8, 2048, 1536], P('dp', 'tp')
All inputs are finite; a program needn't handle non-finite values.
Results may differ from a plain program's by a relative error of at most 0.02.
Values are sent between devices in bfloat16 or wider.
A program may use at most 1 GiB of HBM per device.

v0:
```python
import jax
import jax.numpy as jnp
from jax import lax
from jax.sharding import PartitionSpec as P


def rel_bucket(offsets):
    side = jnp.where(offsets > 0, 16, 0)
    distance = jnp.minimum(jnp.abs(offsets), 128)
    limits = 64 * 2 ** jnp.arange(1, 8)
    steps = jnp.sum((distance[:, None] * distance[:, None] >= limits[None, :]).astype(jnp.int32), axis=1)
    return side + jnp.where(distance < 8, distance, 8 + steps)


def rms_norm(rows_in, gain_vec):
    rows32 = rows_in.astype(jnp.float32)
    inv_rms = lax.rsqrt(jnp.mean(rows32 * rows32, axis=-1, keepdims=True) + 1e-6)
    return (rows32 * inv_rms * gain_vec).astype(jnp.bfloat16)


def bias_rows(dist_table, seq_len, row_start, row_count):
    padded = jnp.pad(dist_table, ((0, 0), (0, 1)))
    doubled = jnp.concatenate([padded, padded], axis=1)
    shifted = lax.dynamic_slice_in_dim(doubled, 2 * seq_len - row_start, 2 * seq_len, axis=1)
    tiled = jnp.tile(shifted, (1, row_count))[:, : row_count * (2 * seq_len - 1)]
    return tiled.reshape(dist_table.shape[0], row_count, 2 * seq_len - 1)[:, :, seq_len - 1:]


def solution(mesh):
    group_size = mesh.shape['tp']
    col_spec = P(None, None, 'tp')
    row_spec = P(None, 'tp', None)

    def local_fn(tokens, pad_mask, rel_table, w_query, w_key, w_value, w_out, w_act, w_lin, w_down, norm_attn, norm_mlp):
        batch, seq_loc, model_dim = tokens.shape
        seq_len = seq_loc * group_size
        head_count = rel_table.shape[1]
        head_dim = w_query.shape[2] // head_count
        offsets = jnp.arange(2 * seq_len - 1) - (seq_len - 1)
        rel_bias = bias_rows(jnp.take(rel_table.T, rel_bucket(offsets), axis=1), seq_len, 0, seq_len)
        key_bias = jnp.where(pad_mask == 1, 0.0, -1e9).astype(jnp.float32)[:, None, None, :]

        def project(gathered, weight_mat):
            projected = jnp.einsum('bsd,dn->bsn', gathered, weight_mat, preferred_element_type=jnp.float32)
            return projected.astype(jnp.bfloat16).reshape(batch, seq_len, head_count, head_dim)

        residual = tokens
        for layer_idx in range(w_query.shape[0]):
            gathered = lax.all_gather(rms_norm(residual, norm_attn[layer_idx]), 'tp', axis=1, tiled=True)
            query_proj = project(gathered, w_query[layer_idx])
            key_proj = project(gathered, w_key[layer_idx])
            value_proj = project(gathered, w_value[layer_idx])
            scores = jnp.einsum('bqhe,bkhe->bhqk', query_proj, key_proj, preferred_element_type=jnp.float32)
            attn_probs = jax.nn.softmax(scores + rel_bias + key_bias, axis=-1).astype(jnp.bfloat16)
            context = jnp.einsum('bhqk,bkhe->bqhe', attn_probs, value_proj, preferred_element_type=jnp.float32).astype(jnp.bfloat16)
            out_mat = w_out[layer_idx].reshape(head_count, head_dim, model_dim)
            part_out = jnp.einsum('crif,ife->cre', context, out_mat, preferred_element_type=jnp.float32).astype(jnp.bfloat16)
            attn_out = lax.psum_scatter(part_out, 'tp', scatter_dimension=1, tiled=True)
            mid_resid = (residual.astype(jnp.float32) + attn_out.astype(jnp.float32)).astype(jnp.bfloat16)
            gathered = lax.all_gather(rms_norm(mid_resid, norm_mlp[layer_idx]), 'tp', axis=1, tiled=True)
            act_proj = jnp.einsum('bsd,df->bsf', gathered, w_act[layer_idx], preferred_element_type=jnp.float32)
            lin_proj = jnp.einsum('bsd,df->bsf', gathered, w_lin[layer_idx], preferred_element_type=jnp.float32)
            gated = (jax.nn.gelu(act_proj, approximate=True) * lin_proj).astype(jnp.bfloat16)
            part_out = jnp.einsum('bsf,fd->bsd', gated, w_down[layer_idx], preferred_element_type=jnp.float32).astype(jnp.bfloat16)
            ffn_out = lax.psum_scatter(part_out, 'tp', scatter_dimension=1, tiled=True)
            residual = (mid_resid.astype(jnp.float32) + ffn_out.astype(jnp.float32)).astype(jnp.bfloat16)
        return residual

    in_specs = (P('dp', 'tp', None), P('dp', None), P(None, 'tp'), col_spec, col_spec, col_spec, row_spec,
                col_spec, col_spec, row_spec, P(None, None), P(None, None))
    return jax.shard_map(local_fn, mesh=mesh, in_specs=in_specs, out_specs=P('dp', 'tp', None), check_vma=False)
```

profile of v0, /device:TPU:0, one launch (start us, length us, event | category | flops | bytes accessed | tf_op | source)
XLA Modules:
  0.0 3302.9 jit_solution(4288171534927202444)
XLA Ops:
  58.9 107.8 %copy.52 = f32[1,2,2048,4096]{3,1,2,0:T(2,128)} copy(f32[1,2,2048,4096]{3,2,1,0:T(8,128)} %broadcast_bitcast_fusion) | data formatting | bytes 134217728
  166.7 44.1 %slice.82 = f32[2,8386560]{1,0:T(2,128)} slice(f32[2,8388608]{1,0:T(2,128)} %bitcast.53), slice={[0:2], [0:8386560]} | slice | bytes 134184960 | tf_op jit(solution)/shard_map/slice | solution.py:25
  210.8 145.3 %reshape.190 = f32[16773120]{0:T(1024)} reshape(f32[2,8386560]{1,0:T(2,128)} %slice.82) | data formatting | bytes 134184960
  356.1 88.3 %reshape.158 = f32[2,2048,4095]{2,1,0:T(8,128)} reshape(f32[16773120]{0:T(1024)} %reshape.190) | data formatting | bytes 134184960 | tf_op jit(solution)/shard_map/reshape | solution.py:26
  444.5 25.8 slice.83
  470.2 33.7 %copy.35 = f32[2,2048,2048]{1,2,0:T(8,128)} copy(f32[2,2048,2048]{2,1,0:T(8,128)} %slice.83) | data formatting | bytes 67108864 | tf_op jit(solution)/shard_map/slice | solution.py:26
  504.9 25.0 convolution_convert_fusion.5
  554.5 199.0 %fusion.97 = (f32[8,2,2048]{2,1,0:T(2,128)S(1)}, f32[8,2,2048,2048]{2,3,1,0:T(8,128)}) fusion(f32[8,2048]{1,0:T(8,128)S(1)} %compare_select_fusion.2, f32[2,2048,2048]{1,2,0:T(8,128)} %copy.35, bf16[8,2048,2,64]{1,3,2,0:T(8,128)(2,1)} %bitcast.145, bf16[8,2048,2,64]{1,3,2,0:T(8,128)(2,1)} %bitcast.144), kind=kOutput, calls=%fused_computation.149 | convolution fusion | flops 8858372096 | bytes 310575104 | tf_op jit(solution)/shard_map/sub | solution.py:54
  753.5 24.6 convolution_convert_fusion.7
  778.1 83.4 %fusion.148 = bf16[8,2048,2,64]{1,3,2,0:T(8,128)(2,1)} fusion(bf16[8,2048,2,64]{1,3,2,0:T(8,128)(2,1)} %bitcast.147, f32[8,2,2048,2048]{2,3,1,0:T(8,128)} %get-tuple-element.14, f32[8,2,2048]{2,1,0:T(2,128)S(1)} %get-tuple-element.13), kind=kOutput, calls=%fused_computation.73.clone | convolution fusion | flops 8726249472 | bytes 276955136 | tf_op jit(solution)/shard_map/bhqk,bkhe->bqhe/dot_general | solution.py:55
  885.5 276.2 %reduce-scatter.5.cloned.1.call-done = bf16[8,256,1536]{2,1,0:T(8,128)(2,1)} async-done(((bf16[8,2048,1536]{2,1,0:T(8,128)(2,1)}), bf16[8,256,1536]{2,1,0:T(8,128)(2,1)}) %reduce-scatter.5.cloned.1.call-update) | async-done | bytes 6291472 | tf_op jit(solution)/shard_map/reduce_scatter | solution.py:58
  1178.3 226.5 %all-gather.7.cloned.1.call-done = bf16[8,2048,1536]{2,1,0:T(8,128)(2,1)} async-done(((bf16[8,256,1536]{2,1,0:T(8,128)(2,1)}), bf16[8,2048,1536]{2,1,0:T(8,128)(2,1)}) %all-gather.7.cloned.1.call-update) | async-done | bytes 50331664 | tf_op jit(solution)/shard_map/all_gather | solution.py:60
  1404.8 34.6 %fusion.57 = f32[8,2048,480]{1,2,0:T(8,128)} fusion(bf16[8,2048,1536]{2,1,0:T(8,128)(2,1)} %all-gather.7.cloned.1.call-done, bf16[2,1536,480]{1,2,0:T(8,128)(2,1)S(1)} %copy-done.17), kind=kOutput, calls=%fused_computation.88 | convolution fusion | flops 24159191040 | bytes 83263488 | tf_op jit(solution)/shard_map/bsd,df->bsf/dot_general | solution.py:62
  1439.4 60.9 %convolution_convert_fusion.1 = bf16[8,2048,1536]{2,1,0:T(8,128)(2,1)} fusion(bf16[2,480,1536]{2,1,0:T(8,128)(2,1)} %param.21, f32[8,2048,480]{1,2,0:T(8,128)} %fusion.57, bf16[8,2048,1536]{2,1,0:T(8,128)(2,1)} %all-gather.7.cloned.1.call-done, bf16[2,1536,480]{1,2,0:T(8,128)(2,1)} %param.19), kind=kOutput, calls=%fused_computation.22 | convolution fusion | flops 48422191104 | bytes 135069696 | tf_op jit(solution)/shard_map/bsf,fd->bsd/dot_general | solution.py:64
  1500.4 274.6 %reduce-scatter.7.cloned.1.call-done = bf16[8,256,1536]{2,1,0:T(8,128)(2,1)} async-done(((bf16[8,2048,1536]{2,1,0:T(8,128)(2,1)}), bf16[8,256,1536]{2,1,0:T(8,128)(2,1)}) %reduce-scatter.7.cloned.1.call-update) | async-done | bytes 6291472 | tf_op jit(solution)/shard_map/reduce_scatter | solution.py:65
  1790.1 226.5 %all-gather.9.cloned.1.call-done = bf16[8,2048,1536]{2,1,0:T(8,128)(2,1)} async-done(((bf16[8,256,1536]{2,1,0:T(8,128)(2,1)}), bf16[8,2048,1536]{2,1,0:T(8,128)(2,1)}) %all-gather.9.cloned.1.call-update) | async-done | bytes 50331664 | tf_op jit(solution)/shard_map/all_gather | solution.py:49
  2016.6 25.0 convolution_convert_fusion.2
  2066.2 199.0 %fusion.98 = (f32[8,2,2048]{2,1,0:T(2,128)S(1)}, f32[8,2,2048,2048]{2,3,1,0:T(8,128)}) fusion(f32[8,2048]{1,0:T(8,128)S(1)} %copy-done.2, f32[2,2048,2048]{1,2,0:T(8,128)} %copy.35, bf16[8,2048,2,64]{1,3,2,0:T(8,128)(2,1)} %bitcast.143, bf16[8,2048,2,64]{1,3,2,0:T(8,128)(2,1)} %bitcast.142), kind=kOutput, calls=%fused_computation.150 | convolution fusion | flops 8858372096 | bytes 310575104 | tf_op jit(solution)/shard_map/sub | solution.py:54
  2289.7 83.4 %fusion.145 = bf16[8,2048,2,64]{1,3,2,0:T(8,128)(2,1)} fusion(bf16[8,2048,2,64]{1,3,2,0:T(8,128)(2,1)} %bitcast.148, f32[8,2,2048,2048]{2,3,1,0:T(8,128)} %get-tuple-element.16, f32[8,2,2048]{2,1,0:T(2,128)S(1)} %get-tuple-element.15), kind=kOutput, calls=%fused_computation.72.clone.1 | convolution fusion | flops 8726249472 | bytes 276955136 | tf_op jit(solution)/shard_map/bhqk,bkhe->bqhe/dot_general | solution.py:55
  2395.9 274.6 %reduce-scatter.9.cloned.1.call-done = bf16[8,256,1536]{2,1,0:T(8,128)(2,1)} async-done(((bf16[8,2048,1536]{2,1,0:T(8,128)(2,1)}), bf16[8,256,1536]{2,1,0:T(8,128)(2,1)}) %reduce-scatter.9.cloned.1.call-update) | async-done | bytes 6291472 | tf_op jit(solution)/shard_map/reduce_scatter | solution.py:58
  2687.1 226.5 %all-gather.11.cloned.1.call-done = bf16[8,2048,1536]{2,1,0:T(8,128)(2,1)} async-done(((bf16[8,256,1536]{2,1,0:T(8,128)(2,1)}), bf16[8,2048,1536]{2,1,0:T(8,128)(2,1)}) %all-gather.11.cloned.1.call-update) | async-done | bytes 50331664 | tf_op jit(solution)/shard_map/all_gather | solution.py:60
  2913.6 34.6 %fusion.53 = f32[8,2048,480]{1,2,0:T(8,128)} fusion(bf16[8,2048,1536]{2,1,0:T(8,128)(2,1)} %all-gather.11.cloned.1.call-done, bf16[2,1536,480]{1,2,0:T(8,128)(2,1)S(1)} %copy-done.18), kind=kOutput, calls=%fused_computation.84 | convolution fusion | flops 24159191040 | bytes 83263488 | tf_op jit(solution)/shard_map/bsd,df->bsf/dot_general | solution.py:62
  2948.2 61.2 %convolution_convert_fusion = bf16[8,2048,1536]{2,1,0:T(8,128)(2,1)} fusion(bf16[2,480,1536]{2,1,0:T(8,128)(2,1)} %param.21, f32[8,2048,480]{1,2,0:T(8,128)} %fusion.53, bf16[8,2048,1536]{2,1,0:T(8,128)(2,1)} %all-gather.11.cloned.1.call-done, bf16[2,1536,480]{1,2,0:T(8,128)(2,1)} %param.19), kind=kOutput, calls=%fused_computation.21 | convolution fusion | flops 48422191104 | bytes 135069696 | tf_op jit(solution)/shard_map/bsf,fd->bsd/dot_general | solution.py:64
  3009.4 274.7 %reduce-scatter.11.cloned.1.call-done = bf16[8,256,1536]{2,1,0:T(8,128)(2,1)} async-done(((bf16[8,2048,1536]{2,1,0:T(8,128)(2,1)}), bf16[8,256,1536]{2,1,0:T(8,128)(2,1)}) %reduce-scatter.11.cloned.1.call-update) | async-done | bytes 6291472 | tf_op jit(solution)/shard_map/reduce_scatter | solution.py:65
  (90 shorter events, 233.5 us)
Async XLA Ops:
  6.5 498.4 %all-gather.5.cloned.1.call-start = ((), (), s32[]{:S(2)}) async-start(), calls=%async_computation.4 | async-start | bytes 56623104 | tf_op jit(solution)/shard_map/all_gather | solution.py:49
  19.1 1142.7 %reduce-scatter.5.cloned.1.call-start = ((), (), s32[]{:S(2)}) async-start(), calls=%async_computation.5 | async-start | bytes 56623104 | tf_op jit(solution)/shard_map/reduce_scatter | solution.py:58
  470.2 33.7 %copy-start.12 = (s32[8,2048]{1,0:T(8,128)S(1)}, s32[8,2048]{1,0:T(8,128)}, u32[]{:S(2)}) copy-start(s32[8,2048]{1,0:T(8,128)} %param.13) | copy-start | bytes 196612
  470.2 33.7 %copy-start.11 = (bf16[2,128,1536]{2,1,0:T(8,128)(2,1)S(1)}, bf16[2,128,1536]{2,1,0:T(8,128)(2,1)}, u32[]{:S(2)}) copy-start(bf16[2,128,1536]{2,1,0:T(8,128)(2,1)} %param.18) | copy-start | bytes 2359300
  470.2 34.7 %copy-start.5 = (bf16[2,1536,128]{2,1,0:T(8,128)(2,1)S(1)}, bf16[2,1536,128]{2,1,0:T(8,128)(2,1)}, u32[]{:S(2)}) copy-start(bf16[2,1536,128]{2,1,0:T(8,128)(2,1)} %param.16) | copy-start | bytes 2359300
  504.0 50.6 %copy-start.1 = (f32[8,2048]{1,0:T(8,128)}, f32[8,2048]{1,0:T(8,128)S(1)}, u32[]{:S(2)}) copy-start(f32[8,2048]{1,0:T(8,128)S(1)} %compare_select_fusion.2) | copy-start | bytes 196612
  504.9 25.0 copy-start.7
  554.5 199.0 %copy-start.9 = (bf16[2,1536,128]{2,1,0:T(8,128)(2,1)S(1)}, bf16[2,1536,128]{2,1,0:T(8,128)(2,1)}, u32[]{:S(2)}) copy-start(bf16[2,1536,128]{2,1,0:T(8,128)(2,1)} %param.17) | copy-start | bytes 2359300
  778.1 83.4 %copy-start.4 = (bf16[1,128,1536]{2,1,0:T(8,128)(2,1)S(1)}, bf16[1,128,1536]{2,1,0:T(8,128)(2,1)}, u32[]{:S(2)}) copy-start(bf16[1,128,1536]{2,1,0:T(8,128)(2,1)} %get-tuple-element.11) | copy-start | bytes 1179652
  884.2 520.6 %all-gather.7.cloned.1.call-start = ((), (), s32[]{:S(2)}) async-start(), calls=%async_computation.6 | async-start | bytes 56623104 | tf_op jit(solution)/shard_map/all_gather | solution.py:60
  1168.5 236.3 %copy-start.17 = (bf16[2,1536,480]{1,2,0:T(8,128)(2,1)S(1)}, bf16[2,1536,480]{1,2,0:T(8,128)(2,1)}, u32[]{:S(2)}) copy-start(bf16[2,1536,480]{1,2,0:T(8,128)(2,1)} %param.20) | copy-start | bytes 8847364
  1178.2 596.8 %reduce-scatter.7.cloned.1.call-start = ((), (), s32[]{:S(2)}) async-start(), calls=%async_computation.7 | async-start | bytes 56623104 | tf_op jit(solution)/shard_map/reduce_scatter | solution.py:65
  1500.3 285.5 %copy-start.13 = (f32[1536]{0:T(1024)S(1)}, f32[1536]{0:T(1024)}, u32[]{:S(2)}) copy-start(f32[1536]{0:T(1024)} %get-tuple-element.5) | copy-start | bytes 18436
  1500.3 516.3 %all-gather.9.cloned.1.call-start = ((), (), s32[]{:S(2)}) async-start(), calls=%async_computation.8 | async-start | bytes 56623104 | tf_op jit(solution)/shard_map/all_gather | solution.py:49
  1783.1 233.5 %copy-start.6 = (bf16[2,1536,128]{2,1,0:T(8,128)(2,1)S(1)}, bf16[2,1536,128]{2,1,0:T(8,128)(2,1)}, u32[]{:S(2)}) copy-start(bf16[2,1536,128]{2,1,0:T(8,128)(2,1)} %param.16) | copy-start | bytes 2359300
  1790.0 251.6 %copy-start.8 = (bf16[2,1536,128]{2,1,0:T(8,128)(2,1)S(1)}, bf16[2,1536,128]{2,1,0:T(8,128)(2,1)}, u32[]{:S(2)}) copy-start(bf16[2,1536,128]{2,1,0:T(8,128)(2,1)} %param.15) | copy-start | bytes 2359300
  1790.0 880.5 %reduce-scatter.9.cloned.1.call-start = ((), (), s32[]{:S(2)}) async-start(), calls=%async_computation.9 | async-start | bytes 56623104 | tf_op jit(solution)/shard_map/reduce_scatter | solution.py:58
  2041.6 24.6 copy-start.2
  2066.2 199.0 %copy-start.10 = (bf16[2,1536,128]{2,1,0:T(8,128)(2,1)S(1)}, bf16[2,1536,128]{2,1,0:T(8,128)(2,1)}, u32[]{:S(2)}) copy-start(bf16[2,1536,128]{2,1,0:T(8,128)(2,1)} %param.17) | copy-start | bytes 2359300
  2289.7 83.4 %copy-start.3 = (bf16[1,128,1536]{2,1,0:T(8,128)(2,1)S(1)}, bf16[1,128,1536]{2,1,0:T(8,128)(2,1)}, u32[]{:S(2)}) copy-start(bf16[1,128,1536]{2,1,0:T(8,128)(2,1)} %get-tuple-element.12) | copy-start | bytes 1179652
  2395.9 281.4 %copy-start.14 = (f32[1536]{0:T(1024)S(1)}, f32[1536]{0:T(1024)}, u32[]{:S(2)}) copy-start(f32[1536]{0:T(1024)} %get-tuple-element.8) | copy-start | bytes 18436
  2395.9 517.7 %all-gather.11.cloned.1.call-start = ((), (), s32[]{:S(2)}) async-start(), calls=%async_computation.10 | async-start | bytes 56623104 | tf_op jit(solution)/shard_map/all_gather | solution.py:60
  2677.3 236.3 %copy-start.18 = (bf16[2,1536,480]{1,2,0:T(8,128)(2,1)S(1)}, bf16[2,1536,480]{1,2,0:T(8,128)(2,1)}, u32[]{:S(2)}) copy-start(bf16[2,1536,480]{1,2,0:T(8,128)(2,1)} %param.20) | copy-start | bytes 8847364
  2687.0 597.1 %reduce-scatter.11.cloned.1.call-start = ((), (), s32[]{:S(2)}) async-start(), calls=%async_computation.11 | async-start | bytes 56623104 | tf_op jit(solution)/shard_map/reduce_scatter | solution.py:65
  (3 other events, 16.0 us)
Sparse Core Ops, SparseCore 0:
  19.2 229.2 all-gather.4
  884.3 277.3 reduce-scatter.4
  1178.3 226.4 all-gather.6
  1500.4 274.4 reduce-scatter.6
  1790.1 226.4 all-gather.8
  2396.0 274.4 reduce-scatter.8
  2687.1 226.4 all-gather.10
  3009.5 274.4 reduce-scatter.10
where the time goes:
time: 3310 us; the launch traced here: 3300 us
  waiting for transfers between devices  1780 us (54%)
  matrix products  950 us (29%)
  local copies, waits for them, and re-layouts  487 us (15%)
  other arithmetic  71.8 us (2%)
    reduce_scatter x2, waiting for transfers between devices, local_fn(): attn_out = lax.psum_scatter(part_out, 'tp', scatter_dimension=1, tiled=True)  551 us
    reduce_scatter x2, waiting for transfers between devices, local_fn(): ffn_out = lax.psum_scatter(part_out, 'tp', scatter_dimension=1, tiled=True)  549 us
    all_gather x2, waiting for transfers between devices, local_fn(): lax.all_gather(rms_norm(mid_resid, norm_mlp[layer_idx]), 'tp', axis=1, ti...  453 us
    sub x2, matrix products, local_fn(): jax.nn.softmax(scores + rel_bias + key_bias, axis=-1).astype(jnp.bfloat16)  398 us
    unnamed x43, local copies, waits for them, and re-layouts  278 us
    all_gather x2, waiting for transfers between devices, local_fn(): lax.all_gather(rms_norm(residual, norm_attn[layer_idx]), 'tp', axis=1, ti...  227 us
    dot_general x2, matrix products, local_fn(): jnp.einsum('bhqk,bkhe->bqhe', attn_probs, value_proj, preferred_element_t...  167 us
    dot_general x6, matrix products, project(): jnp.einsum('bsd,dn->bsn', gathered, weight_mat, preferred_element_type=jn...  148 us
  transfers between devices with their start and end apart: 8, of which 7 were waited for; matrix products, arithmetic and copies ran while one was open for 15% of the time, Pallas kernels for 0%

commit v1 on v0

v1 whole, which is shorter than its diff:
```python
import jax
import jax.numpy as jnp
from jax import lax
from jax.experimental import pallas as pl
from jax.experimental.pallas import tpu as pltpu
from jax.sharding import PartitionSpec as P

LOG2E = 1.4426950408889634
MESH = pl.DeviceIdType.MESH
F32, BF16 = jnp.float32, jnp.bfloat16
NT = (((1,), (1,)), ((), ()))

SEQ, DM, NH, NDEV, LAYERS = 2048, 1536, 16, 8, 2
LANES = 128
HD = 64
PART = SEQ // NDEV
KC = 256
NT_K = SEQ // KC
BQ = 512
NB = SEQ // BQ
NSUB = BQ // KC
HROWS = LANES
QROWS = 3 * HROWS
SHARD = 480
FR = 96
NG = SHARD // FR
GF = NDEV * FR
NF = 3 * NG
LEAD = 5
LAG = 5
VMEM_BYTES = 67043328

SEQUENCE = []
for _l in range(LAYERS):
    SEQUENCE += [('q', 3 * _l + i) for i in range(3)] + [('o', _l)] + [('f', NF * _l + i) for i in range(NF)]
NSEQ = len(SEQUENCE)
PER = NSEQ // LAYERS
ROWS = {'q': HROWS, 'o': HROWS, 'f': FR}
EVERY = tuple(range(NDEV))
LATE = (13, 14) + tuple(range(25, 30))
O_SEQ, F_SEQ = 3, 4


def split3(x):
    a = x.astype(BF16).astype(F32)
    b = (x - a).astype(BF16).astype(F32)
    return a, b, x - a - b


def gelu(x):
    return 0.5 * x * (1.0 + jnp.tanh(0.7978845608028654 * (x + 0.044715 * (x * x * x))))


def span(start, size, unit=LANES):
    return pl.ds(pl.multiple_of(start, unit), size)


def start(cps):
    for c in cps:
        c.start()


def wait(cps):
    for c in cps:
        c.wait()


def mega_kernel(tok, pad, rel, wq, wk, wv, wo, wa, wl, wd, n1, n2,
                out, gq, go, gf, xs,
                X, U, B, W, wb, F, Fo, ka_ref, qa_ref, mx, rawq,
                near_q, near_o, near_f, far_q, far_o, far_f, mate_q, mate_o, mate_f, sent_q, sent_o, sent_f,
                ts, tr, fts, ftr, ys, yr, ls, gs, vs, ps, rl):
    me = lax.axis_index('tp')
    core, chip = me % 2, me // 2
    cx, cy = chip % 2, chip // 2
    nx = cy * 4 + (1 - cx) * 2 + core
    ny = (1 - cy) * 4 + cx * 2 + core
    nd = (1 - cy) * 4 + (1 - cx) * 2 + core

    def other(d):
        return d + 1 - 2 * (d % 2)

    mate = other(me)

    def remote(src, dst, ss, rs, dev):
        return pltpu.make_async_remote_copy(src_ref=src, dst_ref=dst, send_sem=ss, recv_sem=rs,
                                            device_id={'tp': dev}, device_id_type=MESH)

    local = pltpu.make_async_copy

    def place(kind, k, owner, r0, r):
        if kind == 'q':
            return gq.at[k // 3, pl.ds(owner * QROWS + (k % 3) * HROWS + r0, r)]
        if kind == 'o':
            return go.at[k, pl.ds(owner * HROWS + r0, r)]
        return gf.at[k, pl.ds(owner * FR + r0, r)]

    def drained(ref, sem):
        local(ref, ref, sem).wait()

    def hop(kind, k, slot):
        r = ROWS[kind]
        owner, r0, rr, dev = ((me, 0, r, nx), (me, 0, r, ny), (me, 0, r, mate), (nx, 0, r // 2, ny),
                              (ny, r // 2, r // 2, nx), (nx, 0, r, mate), (ny, 0, r, mate), (nd, 0, r, mate))[slot]
        ref = place(kind, k, owner, r0, rr)
        near, far, via, sent = {'q': (near_q, far_q, mate_q, sent_q), 'o': (near_o, far_o, mate_o, sent_o),
                                'f': (near_f, far_f, mate_f, sent_f)}[kind]
        if slot < 2:
            got = near.at[k, slot]
        elif slot in (3, 4):
            got = far.at[k // 3 if kind == 'q' else k]
        elif kind == 'q':
            got = via.at[k // 3, max(slot - 4, 0)]
        else:
            got = via.at[k // 3 if kind == 'f' else k]
        return remote(ref, ref, sent.at[k // 3 if kind != 'o' else k], got, dev)

    def send_own(kind, k):
        start(hop(kind, k, slot) for slot in EVERY[:3])

    def forward(kind, k):
        for near in EVERY[:2]:
            hop(kind, k, near).wait_recv()
            start(hop(kind, k, near + step) for step in (3, 5))

    def forward_far(kind, k):
        if kind == 'q':
            drained(gq.at[k // 3, :QROWS], far_q.at[k // 3])
            start(hop(kind, k + i, EVERY[-1]) for i in range(3))
        else:
            drained(place(kind, k, 0, 0, ROWS[kind]), (far_o if kind == 'o' else far_f).at[k])
            hop(kind, k, EVERY[-1]).start()

    def tick(s):
        forward(*SEQUENCE[s])
        if s >= O_SEQ:
            kind, k = SEQUENCE[max(s - LAG, 0)]
            if kind == 'o' or kind == 'f' and k not in LATE:
                forward_far(kind, k)
            if s + LEAD < NSEQ:
                send_own(*SEQUENCE[s + LEAD])

    def tick_f(k):
        forward('f', k)

        @pl.when(k % NF == LAG - 1)
        def _():
            forward_far('o', k // NF)

        @pl.when(k % NF >= LAG)
        def _():
            forward_far('f', k - LAG)

        @pl.when(k < LAYERS * NF - LEAD)
        def _():
            send_own('f', k + LEAD)

    REST = slice(QROWS, BQ + 3 * SHARD)

    def load_raw(l):
        cps = [local(w.at[l], rawq.at[l, i], rl.at[l, 0]) for i, w in enumerate((wq, wk, wv))]
        cps += [local(wo.at[l], B.at[l, QROWS:BQ], rl.at[l, 1])]
        return cps + [local(w.at[l], B.at[l, BQ + SHARD * i:BQ + SHARD * (i + 1)], rl.at[l, 1])
                      for i, w in enumerate((wa, wl, wd))]

    def store_own(l):
        cps = [local(B.at[l, :QROWS], gq.at[l, pl.ds(me * QROWS, QROWS)], ps.at[l, 0]),
               local(B.at[l, QROWS:BQ], go.at[l, pl.ds(me * HROWS, HROWS)], ps.at[l, 1])]
        for m in range(3):
            for g in range(NG):
                r0 = BQ + SHARD * m + FR * g
                cps.append(local(B.at[l, r0:r0 + FR], gf.at[NF * l + 3 * g + m, pl.ds(me * FR, FR)], ps.at[l, 1]))
        return cps

    barrier = pltpu.get_barrier_semaphore()
    for o in EVERY[1:]:
        pl.semaphore_signal(barrier, inc=1, device_id={'tp': (me + o) % NDEV}, device_id_type=MESH)
    stores = [store_own(l) for l in range(LAYERS)]
    for l in range(LAYERS):
        start(load_raw(l))
    pl.semaphore_wait(barrier, NDEV - 1)

    peers = [nd, other(nd), nx, other(nx), ny, other(ny), mate]
    fcp = [remote(Fo, F.at[me], fts.at[0], ftr.at[0], d) for d in peers]
    tcp = [remote(tok.at[d], X.at[pl.ds(me * PART, PART)], ts.at[0], tr.at[i], d) for i, d in enumerate(peers)]
    own_tok = local(tok.at[me], X.at[pl.ds(me * PART, PART)], vs.at[NDEV])
    start((tcp[0], tcp[4], tcp[1], tcp[6], own_tok))

    t = lax.broadcasted_iota(jnp.int32, (1, 4 * KC), 1)
    n = jnp.where(t < 3 * KC, t, t - 4 * KC) - KC
    dist = jnp.minimum(jnp.abs(n), 128)
    steps = sum((dist * dist >= 64 * 2 ** i).astype(jnp.int32) for i in range(1, 8))
    bucket = jnp.where(n > 0, 16, 0) + jnp.where(dist < 8, dist, 8 + steps)
    for h in range(2):
        row = jnp.zeros((1, 4 * KC), F32)
        for b in range(32):
            row = jnp.where(bucket == b, rel[h, b] * LOG2E, row)
        Fo[pl.ds(h, 1), :] = row
    Fo[2:, :] = jnp.zeros((NDEV - 2, 4 * KC), F32)

    for l in range(LAYERS):
        drained(rawq.at[l], rl.at[l, 0])
        for i in range(3):
            for cb in range(DM // LANES):
                at = slice(LANES * cb, LANES * (cb + 1))
                B[l, HROWS * i:HROWS * (i + 1), at] = rawq[l, i, at, :].T
        if l == 0:
            start(fcp)
            start((tcp[5], tcp[2], tcp[3]))
            F[me] = Fo[:, :]
        stores[l][0].start()
        if l == 0:
            stores[l][0].wait()
            for k in range(O_SEQ):
                send_own('q', k)
        drained(B.at[l, REST], rl.at[l, 1])
        start(stores[l][1:])

    m3 = split3(jnp.where(pad[pl.ds(me, 1), :] == 1, 0.0, -1e9).astype(F32) * LOG2E)
    rowi = lax.broadcasted_iota(jnp.int32, (LANES, 1), 0) % HD
    for c in range(NT_K):
        col = slice(c * KC, (c + 1) * KC)
        v = jnp.where(jnp.logical_and(rowi >= 3 * c, rowi < 3 * c + 3), 1.0, jnp.zeros((LANES, KC), F32))
        for p in range(3):
            v = jnp.where(rowi == 3 * NT_K + p, m3[p][:, col], v)
        ka_ref[:, col] = v.astype(BF16)

    drained(F.at[:NDEV - 1], fts.at[0])
    drained(F.at[:NDEV - 1], ftr.at[0])
    lane8 = lax.broadcasted_iota(jnp.int32, (NT_K, LANES), 1) % HD
    qrow8 = lax.broadcasted_iota(jnp.int32, (NT_K, LANES), 0)

    @pl.loop(0, NH)
    def _(h):
        row = F[h // 2, pl.ds(h % 2, 1), :]
        full = pltpu.roll(jnp.broadcast_to(row, (KC, 4 * KC)), 0, 1, stride=1, stride_axis=0)
        for d in range(3):
            W[h, d] = full[:, d * KC:(d + 1) * KC]
        left, right = split3(row[:, :1]), split3(row[:, 2 * KC:2 * KC + 1])
        v = jnp.where(lane8 - 3 * NT_K < 3, 1.0, 0.0)
        for c in range(NT_K):
            for p in range(3):
                far = jnp.where(qrow8 <= c - 2, right[p], jnp.where(qrow8 >= c + 2, left[p], 0.0))
                v = jnp.where(lane8 == 3 * c + p, far, v)
        qa_ref[h] = jnp.where(lane8 < 3 * NT_K + 3, v, 0.0)

    stores[1][0].wait()
    for l in range(LAYERS):
        drained(B.at[l, REST], ps.at[l, 1])

    def norm_rows(src, r0, rows, gain):
        @pl.loop(0, rows // HD)
        def _(i):
            r = span(r0 + i * HD, HD, HD)
            v = src[r, :].astype(F32)
            inv = lax.rsqrt(jnp.mean(v * v, axis=-1, keepdims=True) + 1e-6)
            X[r, :] = (v * inv * gain).astype(BF16)

    def save(d, i):
        r = pl.ds(d * PART, PART)
        return local(X.at[r], xs.at[r], vs.at[i])

    def q_cols(pair):
        return span(pair * LANES, LANES)

    def v_cols(pair):
        return span(1024 * (1 - pair // 4) + LANES * (pair % 4), LANES)

    def k_at(pair, key, size):
        half = SEQ // 2
        return span((key // half) * half + pair * LANES, LANES), span(BQ + key % half, size)

    def qkv_step(p, slot):
        @pl.loop(0, NB)
        def _(m):
            rows = span(m * BQ, BQ)
            res = lax.dot_general(X[rows, :], wb[slot], NT, preferred_element_type=F32)
            for o in range(2):
                pair = 2 * p + o
                q, k, v = (res[:, QROWS * o + LANES * i:QROWS * o + LANES * (i + 1)] for i in range(3))
                B[0, rows, q_cols(pair)] = q.astype(BF16)
                kr, kc = k_at(pair, m * BQ, BQ)
                B[1, kr, kc] = k.T.astype(BF16)
                B[p // 2, rows, v_cols(pair)] = v.astype(BF16)

    def qkv(l):
        order = [chip, nx // 2, ny // 2, nd // 2]
        loads = [local(gq.at[l, pl.ds(p * GF, GF)], wb.at[i % 2], ls.at[i % 2]) for i, p in enumerate(order)]

        def fetch(i):
            if i == 1:
                if l == 0:
                    for s in range(O_SEQ):
                        tick(s)
                    for s in range(O_SEQ, O_SEQ + LEAD):
                        send_own(*SEQUENCE[s])
            if l == 1 and i > 0:
                tick(PER + O_SEQ + i)
            if i == 3:
                forward_far('q', O_SEQ * l)
            drained(gq.at[l, :QROWS], mate_q.at[l, i])
            loads[i].start()

        early = (2,) if l == 0 else (1, 2, 3)
        fetch(0)
        for i, p in enumerate(order):
            loads[i].wait()
            if i + 1 in early:
                fetch(i + 1)
            qkv_step(p, i % 2)
            if i + 1 < NB and i + 1 not in early:
                fetch(i + 1)
        tick((O_SEQ, PER + F_SEQ + 3)[l])

    lane = lax.broadcasted_iota(jnp.int32, (1, LANES), 1)
    krow = lax.broadcasted_iota(jnp.int32, (LANES, 1), 0)
    NU = NH * NB
    ones = jnp.ones((KC, LANES), BF16)

    def sblock(slot, t):
        b = slot * NT_K + t
        wide = DM // KC
        return (b // wide) * BQ, (b % wide) * KC

    def parts(u):
        h = u // NB
        return h, u % NB, h // 2, h % 2

    def tile_at(i, t):
        return (i * NSUB - 1 + t + NT_K) % NT_K

    def q_operand(u):
        h, i, pair, odd = parts(u)
        q32 = B[0, span(i * BQ, BQ), q_cols(pair)].astype(F32) * LOG2E
        hi = q32.astype(BF16).astype(F32)
        mine = (lane // HD) == odd
        qa = jnp.concatenate([jnp.broadcast_to(qa_ref[h, pl.ds(i * NSUB + r, 1), :], (KC, LANES)) for r in range(NSUB)])
        return jnp.concatenate([jnp.where(mine, hi, 0.0).astype(BF16), jnp.where(mine, q32 - hi, qa).astype(BF16)], axis=1)

    def score_tile(u, qv, t, slot, m):
        h, i, pair, odd = parts(u)
        c = tile_at(i, t)
        kr, kc = k_at(pair, c * KC, KC)
        kp = B[1, kr, kc]
        kx = ka_ref[:, span(c * KC, KC)]
        sel = jnp.where((krow // HD) == odd, kp.astype(F32), kx.astype(F32)).astype(BF16)
        s = jnp.dot(qv, jnp.concatenate([kp, sel]), preferred_element_type=F32)
        r0, c0 = sblock(slot, t)
        ms = []
        for r in range(NSUB):
            sr = s[r * KC:(r + 1) * KC]
            d = t - r
            if 0 <= d < 3:
                w = W[h, d]
                if (d, r) in ((0, 0), (2, NSUB - 1)):
                    at = i * NSUB + r - 1 + d
                    w = jnp.where(jnp.logical_and(at >= 0, at < NT_K), w, 0.0)
                sr = sr + w
            U[r0 + r * KC:r0 + (r + 1) * KC, c0:c0 + KC] = sr
            mm = jnp.maximum(sr[:, :LANES], sr[:, LANES:])
            ms.append(jnp.maximum(m[r], mm) if m else mm)
        return ms

    def value_tile(u, t, slot, mr, acc):
        h, i, pair, odd = parts(u)
        r0, c0 = sblock(slot, t)
        p = jnp.exp2(U[r0:r0 + BQ, c0:c0 + KC] - mr).astype(BF16)
        v = B[pair // 4, span(tile_at(i, t) * KC, KC), v_cols(pair)]
        a = jnp.dot(p, jnp.concatenate([v, ones], axis=1), preferred_element_type=F32)
        return a if t == 0 else acc + a

    def row_max(m, slot):
        for r in range(NSUB):
            mx[slot, r * KC:(r + 1) * KC] = jnp.broadcast_to(jnp.max(m[r], axis=1, keepdims=True), (KC, LANES))

    def context(u, acc):
        h, i, pair, odd = parts(u)
        rows, col = span(i * BQ, BQ), q_cols(pair)
        res = acc[:, :LANES] / acc[:, LANES:]
        B[0, rows, col] = jnp.where((lane // HD) == odd, res, B[0, rows, col].astype(F32)).astype(BF16)

    def unit(u, slot):
        nxt = 1 - slot
        un = jnp.minimum(u + 1, NU - 1)
        acc, m = (), ()
        mr = jnp.concatenate([mx[slot], mx[slot]], axis=1)
        qv = q_operand(un)
        for t in range(NT_K):
            m = score_tile(un, qv, t, nxt, m)
            acc = value_tile(u, t, slot, mr, acc)
        row_max(m, nxt)
        context(u, acc)

    def attention(l):
        qv, m = q_operand(0), ()
        for t in range(NT_K):
            m = score_tile(0, qv, t, 0, m)
        row_max(m, 0)

        @pl.loop(0, NU // 2)
        def _(j):
            @pl.when(jnp.logical_and(j % 3 == 0, j < 30))
            def _():
                tick_f((NF + F_SEQ) * l + j // 3)
            for slot in range(2):
                unit(2 * j + slot, slot)

    def out_proj(l):
        @pl.loop(0, NB)
        def _(m):
            rows = span(m * BQ, BQ)
            for nb in range(DM // BQ):
                col = slice(nb * BQ, (nb + 1) * BQ)
                y = jnp.dot(B[0, rows, :GF], wb[0, :, col], preferred_element_type=F32)
                y = y + jnp.dot(B[0, rows, GF:1024], wb[1, :KC, col], preferred_element_type=F32)
                U[rows, col] = (X[rows, col].astype(F32) + y).astype(BF16).astype(F32)

    def load_group(l, g, slot):
        k = NF * l + 3 * g
        to = (B.at[slot, :GF], B.at[slot, GF:2 * GF], wb.at[slot])
        return [local(gf.at[k + i], dst, gs.at[slot]) for i, dst in enumerate(to)]

    def loaded(slot):
        drained(gf.at[:3], gs.at[slot])

    def group_in(l, g):
        drained(gf.at[:3, :4 * FR], mate_f.at[NG * l + g])

    def ffn_step(slot, m):
        rows = span(m * BQ, BQ)
        hm = X[rows, :]
        a = lax.dot_general(hm, B[slot, :GF, :], NT, preferred_element_type=F32)
        b = lax.dot_general(hm, B[slot, GF:2 * GF, :], NT, preferred_element_type=F32)
        g = (gelu(a) * b).astype(BF16)
        U[rows, :] += jnp.dot(g, wb[slot], preferred_element_type=F32)

    def all_sent(l):
        drained(gq.at[l, :7 * QROWS], sent_q.at[l])
        drained(go.at[l, :7 * HROWS], sent_o.at[l])

        @pl.loop(NG * l, NG * (l + 1))
        def _(g):
            drained(gf.at[:3, :7 * FR], sent_f.at[g])

    def block(mi):
        return 2 * ((cy + (mi + 1) % 2) % 2) + (cx + 1 - mi // 2) % 2

    def home(mi, half):
        dev = 2 * block(mi) + half
        return remote(X.at[pl.ds(dev * PART, PART)], out.at[me], ys.at[0], yr.at[0], dev)

    def deliver(mi):
        rows = span(block(mi) * BQ, BQ)
        X[rows, :] = U[rows, :].astype(BF16)
        start(home(mi, half) for half in range(2))

    seen = [(me, own_tok), (mate, tcp[6]), (ny, tcp[4]), (other(ny), tcp[5]), (nd, tcp[0]), (other(nd), tcp[1]),
            (nx, tcp[2]), (other(nx), tcp[3])]
    back = [local(xs, X, vs.at[NDEV])]
    for l in range(LAYERS):
        gain1, gain2 = n1[pl.ds(l, 1), :], n2[pl.ds(l, 1), :]
        if l == 0:
            for i, (d, c) in enumerate(seen):
                if i == 0:
                    c.wait()
                else:
                    c.wait_recv()
                save(d, i).start()
                if i > 0:
                    e = seen[i - 1][0]
                    save(e, i - 1).wait()
                    norm_rows(X, e * PART, PART, gain1)
            save(d, i).wait()
            norm_rows(X, d * PART, PART, gain1)
        else:
            for i in EVERY:
                r = slice(i * PART, (i + 1) * PART)
                X[r, :] = U[r, :].astype(BF16)
                save(i, i).start()
            for i in EVERY:
                save(i, i).wait()
                norm_rows(X, i * PART, PART, gain1)
        qkv(l)
        start(back)
        attention(l)
        wait(back)
        drained(go.at[l, :4 * HROWS], mate_o.at[l])
        load_out = [local(go.at[l, :GF], wb.at[0], ls.at[0]), local(go.at[l, GF:], wb.at[1, :KC], ls.at[1])]
        start(load_out)
        tick((14, NSEQ - 1)[l])
        wait(load_out)
        group_in(l, 0)
        first = load_group(l, 0, 1)
        start(first[:2])
        out_proj(l)
        first[2].start()
        if l == 0:
            tick(NF)
        norm_rows(U, 0, SEQ, gain2)

        if l == 0:
            loaded(1)

            @pl.loop(0, NG * NB)
            def _(s):
                g, m = s // NB, s % NB
                for i in EVERY[:-1]:
                    @pl.when(s == (17 * i) // 6)
                    def _():
                        tick(16 + i)

                @pl.when(jnp.logical_and(m == 0, g > 0))
                def _():
                    loaded((g + 1) % 2)

                @pl.when(s == NB * (NG - 1) - 1)
                def _():
                    for k in LATE[:2]:
                        forward_far('f', k)

                @pl.when(jnp.logical_and(m == NB - 1, g < NG - 1))
                def _():
                    group_in(l, g + 1)
                    start(load_group(l, g + 1, g % 2))
                ffn_step((g + 1) % 2, m)
            all_sent(l)
            continue

        @pl.loop(0, NB * NG)
        def _(s):
            mi, g, slot = s // NG, s % NG, (s + 1) % 2
            loaded(slot)

            @pl.when(s == 2)
            def _():
                for k in LATE[2:4]:
                    forward_far('f', k)

            @pl.when(s == 3)
            def _():
                for k in LATE[4:]:
                    forward_far('f', k)

            @pl.when(s < NG - 1)
            def _():
                group_in(l, g + 1)

            @pl.when(s < NB * NG - 1)
            def _():
                start(load_group(l, (g + 1) % NG, 1 - slot))
            ffn_step(slot, block(mi))

            @pl.when(s == NG)
            def _():
                all_sent(l)

            @pl.when(jnp.logical_and(g == NG - 1, mi < NB - 1))
            def _():
                deliver(mi)

    own = span(chip * BQ, BQ)
    X[own, :] = U[own, :].astype(BF16)
    to_mate = remote(X.at[pl.ds(mate * PART, PART)], out.at[me], ys.at[0], yr.at[0], mate)
    to_self = local(X.at[pl.ds(me * PART, PART)], out.at[me], vs.at[NDEV])
    start((to_mate, to_self))
    drained(tok.at[:NDEV - 1], ts.at[0])
    drained(out.at[:NDEV - 1], ys.at[0])
    drained(out.at[:NDEV - 1], yr.at[0])
    to_self.wait()


def solution(mesh):
    col_spec = P(None, None, 'tp')
    row_spec = P(None, 'tp', None)

    def local_fn(tokens, pad_mask, rel_table, w_query, w_key, w_value, w_out, w_act, w_lin, w_down, norm_attn, norm_mlp):
        hbm = pl.BlockSpec(memory_space=pltpu.MemorySpace.HBM)
        vmem = pl.BlockSpec(memory_space=pltpu.VMEM)
        sem = pltpu.SemaphoreType.DMA
        shapes = [(NDEV, PART, DM), (LAYERS, NDEV * QROWS, DM), (LAYERS, NDEV * HROWS, DM), (LAYERS * NF, GF, DM), (SEQ, DM)]
        chunks = (O_SEQ * LAYERS, LAYERS, LAYERS * NF)
        return pl.pallas_call(
            mega_kernel,
            in_specs=[hbm, vmem, pl.BlockSpec(memory_space=pltpu.SMEM)] + [hbm] * 7 + [vmem] * 2,
            out_specs=[hbm] * 5,
            out_shape=[jax.ShapeDtypeStruct(s, BF16) for s in shapes],
            scratch_shapes=[
                pltpu.VMEM((SEQ, DM), BF16), pltpu.VMEM((SEQ, DM), F32), pltpu.VMEM((2, SEQ, DM), BF16),
                pltpu.VMEM((NH, 3, KC, KC), F32), pltpu.VMEM((2, GF, DM), BF16), pltpu.VMEM((NDEV, NDEV, 4 * KC), F32),
                pltpu.VMEM((NDEV, 4 * KC), F32), pltpu.VMEM((LANES, SEQ), BF16), pltpu.VMEM((NH, NT_K, LANES), F32),
                pltpu.VMEM((2, BQ, LANES), F32), pltpu.VMEM((LAYERS, 3, DM, LANES), BF16),
            ] + [sem((n, 2)) for n in chunks] + [sem((LAYERS,)), sem((LAYERS,)), sem((LAYERS * NF,))] + [
                sem((LAYERS, 4)), sem((LAYERS,)), sem((LAYERS * NG,)), sem((LAYERS,)), sem((LAYERS,)), sem((LAYERS * NG,)),
                sem((1,)), sem((NDEV,))] + [sem((1,))] * 4 + [
                sem((2,)), sem((2,)), sem((NDEV + 1,)), sem((LAYERS, 2)), sem((LAYERS, 2))],
            compiler_params=pltpu.CompilerParams(collective_id=0, has_side_effects=True, vmem_limit_bytes=VMEM_BYTES),
        )(tokens, pad_mask, rel_table.T, w_query, w_key, w_value, w_out, jnp.swapaxes(w_act, 1, 2), jnp.swapaxes(w_lin, 1, 2),
          w_down, norm_attn, norm_mlp)[0]

    in_specs = (P('dp', 'tp', None), P('dp', None), P(None, 'tp'), col_spec, col_spec, col_spec, row_spec,
                col_spec, col_spec, row_spec, P(None, None), P(None, None))
    return jax.shard_map(local_fn, mesh=mesh, in_specs=in_specs, out_specs=P('dp', 'tp', None), check_vma=False)
```

time: 3310 us -> 570 us (0.17)
  waiting for transfers between devices: 1780 us -> 0 us
  matrix products: 950 us -> 0 us
  Pallas kernels: 0 us -> 563 us
  local copies, waits for them, and re-layouts: 487 us -> 5.89 us
  other arithmetic: 71.8 us -> 0 us
    reduce_scatter x4 -> x0, waiting for transfers between devices: 1100 us -> none  [the longest x2 551 us: local_fn(): attn_out = lax.psum_scatter(part_out, 'tp', scatter_dimension=1, tiled=True)]
    all_gather x4 -> x0, waiting for transfers between devices: 680 us -> none  [the longest x2 453 us: local_fn(): lax.all_gather(rms_norm(mid_resid, norm_mlp[layer_idx]), 'tp', axis=1, ti...]
    pallas_call x0 -> x1, Pallas kernels: none -> 563 us  [local_fn(): pl.pallas_call(mega_kernel, in_specs=[hbm, vmem, pl.BlockSpec(memory_spac...]
    dot_general x14 -> x0, matrix products: 552 us -> none  [the longest x2 167 us: local_fn(): jnp.einsum('bhqk,bkhe->bqhe', attn_probs, value_proj, preferred_element_t...]
    sub x2 -> x0, matrix products: 398 us -> none  [local_fn(): jax.nn.softmax(scores + rel_bias + key_bias, axis=-1).astype(jnp.bfloat16)]
    unnamed x43 -> x1, local copies, waits for them, and re-layouts: 278 us -> 5.89 us
    slice x6 -> x0, local copies, waits for them, and re-layouts: 107 us -> none  [the longest x2 59.5 us: bias_rows(): tiled.reshape(dist_table.shape[0], row_count, 2 * seq_len - 1)]
    reshape x1 -> x0, local copies, waits for them, and re-layouts: 88.3 us -> none  [bias_rows(): tiled.reshape(dist_table.shape[0], row_count, 2 * seq_len - 1)]
  transfers between devices with their start and end apart: 8 -> 0, of which waited for: 7 -> 0; matrix products, arithmetic and copies ran while one was open for 15% -> 0% of each run, Pallas kernels for 0% -> 0%
where the time goes in v1:
time: 570 us; the launch traced here: 569 us
  Pallas kernels  563 us (99%)
  local copies, waits for them, and re-layouts  5.89 us (1%)
    pallas_call x1, Pallas kernels, local_fn(): pl.pallas_call(mega_kernel, in_specs=[hbm, vmem, pl.BlockSpec(memory_spac...  563 us

profile of v1, /device:TPU:0, one launch (start us, length us, event | category | flops | bytes accessed | tf_op | source)
XLA Modules:
  0.0 569.2 jit_solution(8500308643682251698)
XLA Ops:
  0.0 563.3 %shard_map.118 = (bf16[8,256,1536]{2,1,0:T(8,128)(2,1)}, bf16[2,3072,1536]{2,1,0:T(8,128)(2,1)}, bf16[2,1024,1536]{2,1,0:T(8,128)(2,1)}, bf16[30,768,1536]{2,1,0:T(8,128)(2,1)}, bf16[2048,1536]{1,0:T(8,128)(2,1)}) custom-call(bf16[8,256,1536]{2,1,0:T(8,128)(2,1)} %tok.1, s32[8,2048]{1,0:T(8,128)} %pad.1, f32[2,32]{1,0:T(2,128)} %bitcast.5, ...), custom_call_target="tpu_custom_call" | custom-call | tf_op jit(solution)/shard_map/pallas_call | solution.py:582
  563.3 5.9 %copy.14 = bf16[8,256,1536]{2,1,0:T(8,128)(2,1)} copy(bf16[8,256,1536]{2,1,0:T(8,128)(2,1)} %get-tuple-element.6) | data formatting | bytes 12582912

commit v2 on v1

--- a/solution.py
+++ b/solution.py
@@ -37,8 +37,13 @@
 PER = NSEQ // LAYERS
 ROWS = {'q': HROWS, 'o': HROWS, 'f': FR}
 EVERY = tuple(range(NDEV))
-LATE = (13, 14) + tuple(range(25, 30))
+LATE = tuple(range(9, 15)) + tuple(range(25, 30))
 O_SEQ, F_SEQ = 3, 4
+
+
+def sent_after(s):
+    held = {14: 18, 15: 18, 16: 19, 17: 20, 18: 22, 19: 22, 20: 23}
+    return held.get(s, min(s + LEAD, NSEQ - 1))
 
 
 def split3(x):
@@ -67,7 +72,7 @@
 
 def mega_kernel(tok, pad, rel, wq, wk, wv, wo, wa, wl, wd, n1, n2,
                 out, gq, go, gf, xs,
-                X, U, B, W, wb, F, Fo, ka_ref, qa_ref, mx, rawq,
+                X, U, B, W, wb, wo2, F, Fo, ka_ref, qa_ref, mx, rawq,
                 near_q, near_o, near_f, far_q, far_o, far_f, mate_q, mate_o, mate_f, sent_q, sent_o, sent_f,
                 ts, tr, fts, ftr, ys, yr, ls, gs, vs, ps, rl):
     me = lax.axis_index('tp')
@@ -112,7 +117,7 @@
         elif kind == 'q':
             got = via.at[k // 3, max(slot - 4, 0)]
         else:
-            got = via.at[k // 3 if kind == 'f' else k]
+            got = via.at[k // 3 + k // (LAYERS * NF - 1) if kind == 'f' else k]
         return remote(ref, ref, sent.at[k // 3 if kind != 'o' else k], got, dev)
 
     def send_own(kind, k):
@@ -137,10 +142,10 @@
             kind, k = SEQUENCE[max(s - LAG, 0)]
             if kind == 'o' or kind == 'f' and k not in LATE:
                 forward_far(kind, k)
-            if s + LEAD < NSEQ:
-                send_own(*SEQUENCE[s + LEAD])
-
-    def tick_f(k):
+            for ahead in range(sent_after(s - 1) + 1, sent_after(s) + 1):
+                send_own(*SEQUENCE[ahead])
+
+    def tick_f(l, k):
         forward('f', k)
 
         @pl.when(k % NF == LAG - 1)
@@ -151,7 +156,7 @@
         def _():
             forward_far('f', k - LAG)
 
-        @pl.when(k < LAYERS * NF - LEAD)
+        @pl.when(k < NF * (l + 1) - LEAD)
         def _():
             send_own('f', k + LEAD)
 
@@ -184,7 +189,7 @@
     fcp = [remote(Fo, F.at[me], fts.at[0], ftr.at[0], d) for d in peers]
     tcp = [remote(tok.at[d], X.at[pl.ds(me * PART, PART)], ts.at[0], tr.at[i], d) for i, d in enumerate(peers)]
     own_tok = local(tok.at[me], X.at[pl.ds(me * PART, PART)], vs.at[NDEV])
-    start((tcp[0], tcp[4], tcp[1], tcp[6], own_tok))
+    start((*tcp[2:], own_tok))
 
     t = lax.broadcasted_iota(jnp.int32, (1, 4 * KC), 1)
     n = jnp.where(t < 3 * KC, t, t - 4 * KC) - KC
@@ -206,7 +211,7 @@
                 B[l, HROWS * i:HROWS * (i + 1), at] = rawq[l, i, at, :].T
         if l == 0:
             start(fcp)
-            start((tcp[5], tcp[2], tcp[3]))
+            start(tcp[:2])
             F[me] = Fo[:, :]
         stores[l][0].start()
         if l == 0:
@@ -296,17 +301,19 @@
                         send_own(*SEQUENCE[s])
             if l == 1 and i > 0:
                 tick(PER + O_SEQ + i)
-            if i == 3:
-                forward_far('q', O_SEQ * l)
+            if i == 3 and l == 0:
+                forward_far('q', 0)
             drained(gq.at[l, :QROWS], mate_q.at[l, i])
             loads[i].start()
 
-        early = (2,) if l == 0 else (1, 2, 3)
+        early = (2,) if l == 0 else (1, 2)
         fetch(0)
         for i, p in enumerate(order):
             loads[i].wait()
             if i + 1 in early:
                 fetch(i + 1)
+            if i == 2 and l == 1:
+                forward_far('q', O_SEQ)
             qkv_step(p, i % 2)
             if i + 1 < NB and i + 1 not in early:
                 fetch(i + 1)
@@ -391,6 +398,9 @@
         row_max(m, nxt)
         context(u, acc)
 
+    def load_out(l):
+        return [local(go.at[l, :GF], wb.at[0], ls.at[0]), local(go.at[l, GF:], wo2, ls.at[1])]
+
     def attention(l):
         qv, m = q_operand(0), ()
         for t in range(NT_K):
@@ -399,21 +409,48 @@
 
         @pl.loop(0, NU // 2)
         def _(j):
-            @pl.when(jnp.logical_and(j % 3 == 0, j < 30))
+            due = jnp.logical_and(j % 3 == 0, j < 30) if l == 0 else j % 7 % 4 == 0
+
+            @pl.when(due)
             def _():
-                tick_f((NF + F_SEQ) * l + j // 3)
+                tick_f(l, j // 3 if l == 0 else NF + F_SEQ + (2 * j + 1) // 7)
+
+            @pl.when(j == 30)
+            def _():
+                drained(go.at[l, :4 * HROWS], mate_o.at[l])
+                start(load_out(l))
             for slot in range(2):
                 unit(2 * j + slot, slot)
 
-    def out_proj(l):
-        @pl.loop(0, NB)
+    def norm_block(m, gain, keep=False):
+        for i in range(BQ // HD):
+            r = span(m * BQ + i * HD, HD, HD)
+            v = U[r, :]
+            if keep:
+                x = v.astype(BF16)
+                B[m % 2, 2 * GF + i * HD:2 * GF + (i + 1) * HD, :] = x
+                v = x.astype(F32)
+            inv = lax.rsqrt(jnp.mean(v * v, axis=-1, keepdims=True) + 1e-6)
+            X[r, :] = (v * inv * gain).astype(BF16)
+
+    def kept(m):
+        return local(B.at[m % 2, pl.ds(2 * GF, BQ)], xs.at[pl.ds(m * BQ, BQ)], vs.at[m])
+
+    def out_block(m):
+        rows = span(m * BQ, BQ)
+        for nb in range(DM // BQ):
+            col = slice(nb * BQ, (nb + 1) * BQ)
+            y = jnp.dot(B[0, rows, :GF], wb[0, :, col], preferred_element_type=F32)
+            y = y + jnp.dot(B[0, rows, GF:1024], wo2[:, col], preferred_element_type=F32)
+            U[rows, col] = (X[rows, col].astype(F32) + y).astype(BF16).astype(F32)
+
+    def out_proj(gain):
+        out_block(0)
+
+        @pl.loop(1, NB)
         def _(m):
-            rows = span(m * BQ, BQ)
-            for nb in range(DM // BQ):
-                col = slice(nb * BQ, (nb + 1) * BQ)
-                y = jnp.dot(B[0, rows, :GF], wb[0, :, col], preferred_element_type=F32)
-                y = y + jnp.dot(B[0, rows, GF:1024], wb[1, :KC, col], preferred_element_type=F32)
-                U[rows, col] = (X[rows, col].astype(F32) + y).astype(BF16).astype(F32)
+            out_block(m)
+            norm_block(m - 1, gain)
 
     def load_group(l, g, slot):
         k = NF * l + 3 * g
@@ -426,13 +463,22 @@
     def group_in(l, g):
         drained(gf.at[:3, :4 * FR], mate_f.at[NG * l + g])
 
-    def ffn_step(slot, m):
-        rows = span(m * BQ, BQ)
-        hm = X[rows, :]
+    def gated(slot, devs):
+        hm = jnp.concatenate([X[span(d * PART, PART), :] for d in devs])
         a = lax.dot_general(hm, B[slot, :GF, :], NT, preferred_element_type=F32)
         b = lax.dot_general(hm, B[slot, GF:2 * GF, :], NT, preferred_element_type=F32)
-        g = (gelu(a) * b).astype(BF16)
-        U[rows, :] += jnp.dot(g, wb[slot], preferred_element_type=F32)
+        return (gelu(a) * b).astype(BF16)
+
+    def add_down(slot, devs, g):
+        y = jnp.dot(g, wb[slot], preferred_element_type=F32)
+        for i, d in enumerate(devs):
+            U[span(d * PART, PART), :] += y[i * PART:(i + 1) * PART]
+
+    def ffn_step(slot, devs):
+        add_down(slot, devs, gated(slot, devs))
+
+    def pair_of(m):
+        return 2 * m, 2 * m + 1
 
     def all_sent(l):
         drained(gq.at[l, :7 * QROWS], sent_q.at[l])
@@ -442,20 +488,22 @@
         def _(g):
             drained(gf.at[:3, :7 * FR], sent_f.at[g])
 
-    def block(mi):
-        return 2 * ((cy + (mi + 1) % 2) % 2) + (cx + 1 - mi // 2) % 2
-
-    def home(mi, half):
-        dev = 2 * block(mi) + half
-        return remote(X.at[pl.ds(dev * PART, PART)], out.at[me], ys.at[0], yr.at[0], dev)
-
-    def deliver(mi):
-        rows = span(block(mi) * BQ, BQ)
-        X[rows, :] = U[rows, :].astype(BF16)
-        start(home(mi, half) for half in range(2))
-
-    seen = [(me, own_tok), (mate, tcp[6]), (ny, tcp[4]), (other(ny), tcp[5]), (nd, tcp[0]), (other(nd), tcp[1]),
-            (nx, tcp[2]), (other(nx), tcp[3])]
+    far_pair = pair_of(nd // 2)
+
+    def near_pair(mi):
+        mine = mi // 3
+        return [(1 - mine) * (2 * (near // 2) + mi - 1) + mine * (2 * chip + i) for i, near in enumerate((nx, ny))]
+
+    def home(d):
+        return remote(X.at[pl.ds(d * PART, PART)], out.at[me], ys.at[0], yr.at[0], d)
+
+    def deliver(devs):
+        for d in devs:
+            r = span(d * PART, PART)
+            X[r, :] = U[r, :].astype(BF16)
+        start(home(d) for d in devs)
+
+    seen = [(me, own_tok)] + [(peers[i], tcp[i]) for i in reversed(range(NDEV - 1))]
     back = [local(xs, X, vs.at[NDEV])]
     for l in range(LAYERS):
         gain1, gain2 = n1[pl.ds(l, 1), :], n2[pl.ds(l, 1), :]
@@ -473,39 +521,29 @@
             save(d, i).wait()
             norm_rows(X, d * PART, PART, gain1)
         else:
-            for i in EVERY:
-                r = slice(i * PART, (i + 1) * PART)
-                X[r, :] = U[r, :].astype(BF16)
-                save(i, i).start()
-            for i in EVERY:
-                save(i, i).wait()
-                norm_rows(X, i * PART, PART, gain1)
+            kept(2).wait()
+            kept(3).wait()
         qkv(l)
         start(back)
         attention(l)
         wait(back)
-        drained(go.at[l, :4 * HROWS], mate_o.at[l])
-        load_out = [local(go.at[l, :GF], wb.at[0], ls.at[0]), local(go.at[l, GF:], wb.at[1, :KC], ls.at[1])]
-        start(load_out)
-        tick((14, NSEQ - 1)[l])
-        wait(load_out)
+        wait(load_out(l))
+        tick((14, NSEQ - 2)[l])
         group_in(l, 0)
         first = load_group(l, 0, 1)
-        start(first[:2])
-        out_proj(l)
-        first[2].start()
-        if l == 0:
-            tick(NF)
-        norm_rows(U, 0, SEQ, gain2)
+        start(first)
+        out_proj(gain2)
+        tick((NF, NSEQ - 1)[l])
+        norm_block(NB - 1, gain2)
 
         if l == 0:
             loaded(1)
 
-            @pl.loop(0, NG * NB)
+            @pl.loop(0, NG * NB - NB + 1)
             def _(s):
                 g, m = s // NB, s % NB
-                for i in EVERY[:-1]:
-                    @pl.when(s == (17 * i) // 6)
+                for i in EVERY[:-2]:
+                    @pl.when(s == 3 * i + 1)
                     def _():
                         tick(16 + i)
 
@@ -513,54 +551,85 @@
                 def _():
                     loaded((g + 1) % 2)
 
-                @pl.when(s == NB * (NG - 1) - 1)
-                def _():
-                    for k in LATE[:2]:
-                        forward_far('f', k)
+                for i in range(2):
+                    @pl.when(s == NB * (3 + i) - 2)
+                    def _():
+                        for k in LATE[3 * i:3 * i + 3]:
+                            forward_far('f', k)
 
                 @pl.when(jnp.logical_and(m == NB - 1, g < NG - 1))
                 def _():
                     group_in(l, g + 1)
                     start(load_group(l, g + 1, g % 2))
-                ffn_step((g + 1) % 2, m)
+                ffn_step((g + 1) % 2, pair_of(m))
+            tick(22)
+
+            @pl.loop(1, NB)
+            def _(m):
+                @pl.when(m > 2)
+                def _():
+                    kept(m - 3).wait()
+                ffn_step(1, pair_of(m))
+                norm_block(m - 1, n1[1:, :], True)
+                kept(m - 1).start()
+            kept(1).wait()
+            norm_block(NB - 1, n1[1:, :], True)
+            kept(NB - 1).start()
             all_sent(l)
             continue
 
-        @pl.loop(0, NB * NG)
+        tail = load_group(l, NG - 1, 1)
+
+        @pl.loop(0, NG - 1)
+        def _(s):
+            slot = (s + 1) % 2
+            loaded(slot)
+
+            @pl.when(s == 2)
+            def _():
+                for k in LATE[6:-1]:
+                    forward_far('f', k)
+
+            @pl.when(s < 3)
+            def _():
+                group_in(l, s + 1)
+                start(load_group(l, s + 1, 1 - slot))
+
+            @pl.when(s == 3)
+            def _():
+                drained(gf.at[:2, :4 * FR], mate_f.at[LAYERS * NG - 1])
+                start(tail[:2])
+            ffn_step(slot, far_pair)
+
+        forward_far('f', LATE[-1])
+        start(load_group(l, 0, 0))
+        drained(gf.at[:2], gs.at[1])
+        g = gated(1, far_pair)
+        drained(gf.at[0, :4 * FR], mate_f.at[LAYERS * NG])
+        tail[2].start()
+        tail[2].wait()
+        add_down(1, far_pair, g)
+        deliver(far_pair)
+        all_sent(l)
+
+        @pl.loop(NG, NB * NG)
         def _(s):
             mi, g, slot = s // NG, s % NG, (s + 1) % 2
             loaded(slot)
 
-            @pl.when(s == 2)
-            def _():
-                for k in LATE[2:4]:
-                    forward_far('f', k)
-
-            @pl.when(s == 3)
-            def _():
-                for k in LATE[4:]:
-                    forward_far('f', k)
-
-            @pl.when(s < NG - 1)
-            def _():
-                group_in(l, g + 1)
-
             @pl.when(s < NB * NG - 1)
             def _():
                 start(load_group(l, (g + 1) % NG, 1 - slot))
-            ffn_step(slot, block(mi))
-
-            @pl.when(s == NG)
-            def _():
-                all_sent(l)
+            ffn_step(slot, near_pair(mi))
 
             @pl.when(jnp.logical_and(g == NG - 1, mi < NB - 1))
             def _():
-                deliver(mi)
-
-    own = span(chip * BQ, BQ)
-    X[own, :] = U[own, :].astype(BF16)
-    to_mate = remote(X.at[pl.ds(mate * PART, PART)], out.at[me], ys.at[0], yr.at[0], mate)
+                deliver(near_pair(mi))
+
+    for d in (mate, me):
+        r = span(d * PART, PART)
+        X[r, :] = U[r, :].astype(BF16)
+    to_mate = home(mate)
     to_self = local(X.at[pl.ds(me * PART, PART)], out.at[me], vs.at[NDEV])
     start((to_mate, to_self))
     drained(tok.at[:NDEV - 1], ts.at[0])
@@ -586,11 +655,11 @@
             out_shape=[jax.ShapeDtypeStruct(s, BF16) for s in shapes],
             scratch_shapes=[
                 pltpu.VMEM((SEQ, DM), BF16), pltpu.VMEM((SEQ, DM), F32), pltpu.VMEM((2, SEQ, DM), BF16),
-                pltpu.VMEM((NH, 3, KC, KC), F32), pltpu.VMEM((2, GF, DM), BF16), pltpu.VMEM((NDEV, NDEV, 4 * KC), F32),
+                pltpu.VMEM((NH, 3, KC, KC), F32), pltpu.VMEM((2, GF, DM), BF16), pltpu.VMEM((KC, DM), BF16), pltpu.VMEM((NDEV, NDEV, 4 * KC), F32),
                 pltpu.VMEM((NDEV, 4 * KC), F32), pltpu.VMEM((LANES, SEQ), BF16), pltpu.VMEM((NH, NT_K, LANES), F32),
                 pltpu.VMEM((2, BQ, LANES), F32), pltpu.VMEM((LAYERS, 3, DM, LANES), BF16),
             ] + [sem((n, 2)) for n in chunks] + [sem((LAYERS,)), sem((LAYERS,)), sem((LAYERS * NF,))] + [
-                sem((LAYERS, 4)), sem((LAYERS,)), sem((LAYERS * NG,)), sem((LAYERS,)), sem((LAYERS,)), sem((LAYERS * NG,)),
+                sem((LAYERS, 4)), sem((LAYERS,)), sem((LAYERS * NG + 1,)), sem((LAYERS,)), sem((LAYERS,)), sem((LAYERS * NG,)),
                 sem((1,)), sem((NDEV,))] + [sem((1,))] * 4 + [
                 sem((2,)), sem((2,)), sem((NDEV + 1,)), sem((LAYERS, 2)), sem((LAYERS, 2))],
             compiler_params=pltpu.CompilerParams(collective_id=0, has_side_effects=True, vmem_limit_bytes=VMEM_BYTES),

time: 570 us -> 560 us (0.982); the launches traced: 569 us -> 551 us
  Pallas kernels: 563 us -> 544 us
    pallas_call x1, Pallas kernels: 563 us -> 544 us  [local_fn(): pl.pallas_call(mega_kernel, in_specs=[hbm, vmem, pl.BlockSpec(memory_spac...]
where the time goes in v2:
time: 560 us; the launch traced here: 551 us
  Pallas kernels  544 us (97%)
  local copies, waits for them, and re-layouts  5.89 us (1%)
    pallas_call x1, Pallas kernels, local_fn(): pl.pallas_call(mega_kernel, in_specs=[hbm, vmem, pl.BlockSpec(memory_spac...  544 us

profile of v2, /device:TPU:0, one launch (start us, length us, event | category | flops | bytes accessed | tf_op | source)
XLA Modules:
  0.0 550.7 jit_solution(1204215502789564254)
XLA Ops:
  0.0 544.3 %shard_map.118 = (bf16[8,256,1536]{2,1,0:T(8,128)(2,1)}, bf16[2,3072,1536]{2,1,0:T(8,128)(2,1)}, bf16[2,1024,1536]{2,1,0:T(8,128)(2,1)}, bf16[30,768,1536]{2,1,0:T(8,128)(2,1)}, bf16[2048,1536]{1,0:T(8,128)(2,1)}) custom-call(bf16[8,256,1536]{2,1,0:T(8,128)(2,1)} %tok.1, s32[8,2048]{1,0:T(8,128)} %pad.1, f32[2,32]{1,0:T(2,128)} %bitcast.5, ...), custom_call_target="tpu_custom_call" | custom-call | tf_op jit(solution)/shard_map/pallas_call | solution.py:651
  544.3 5.9 %copy.14 = bf16[8,256,1536]{2,1,0:T(8,128)(2,1)} copy(bf16[8,256,1536]{2,1,0:T(8,128)(2,1)} %get-tuple-element.6) | data formatting | bytes 12582912

commit v3 on v2

--- a/solution.py
+++ b/solution.py
@@ -289,34 +289,45 @@
                 B[p // 2, rows, v_cols(pair)] = v.astype(BF16)
 
     def qkv(l):
-        order = [chip, nx // 2, ny // 2, nd // 2]
-        loads = [local(gq.at[l, pl.ds(p * GF, GF)], wb.at[i % 2], ls.at[i % 2]) for i, p in enumerate(order)]
+        def load(i):
+            p, slot = 2 * ((cy + i // 2) % 2) + (cx + i % 2) % 2, i % 2
+            return p, slot, local(gq.at[l, pl.ds(p * GF, GF)], wb.at[slot], ls.at[slot])
 
         def fetch(i):
-            if i == 1:
-                if l == 0:
-                    for s in range(O_SEQ):
-                        tick(s)
-                    for s in range(O_SEQ, O_SEQ + LEAD):
-                        send_own(*SEQUENCE[s])
-            if l == 1 and i > 0:
+            if i == 1 and l == 0:
+                for s in range(O_SEQ):
+                    tick(s)
+                for s in range(O_SEQ, O_SEQ + LEAD):
+                    send_own(*SEQUENCE[s])
+            if l == 1:
                 tick(PER + O_SEQ + i)
             if i == 3 and l == 0:
                 forward_far('q', 0)
             drained(gq.at[l, :QROWS], mate_q.at[l, i])
-            loads[i].start()
-
-        early = (2,) if l == 0 else (1, 2)
-        fetch(0)
-        for i, p in enumerate(order):
-            loads[i].wait()
-            if i + 1 in early:
-                fetch(i + 1)
-            if i == 2 and l == 1:
-                forward_far('q', O_SEQ)
-            qkv_step(p, i % 2)
-            if i + 1 < NB and i + 1 not in early:
-                fetch(i + 1)
+            load(i)[2].start()
+
+        drained(gq.at[l, :QROWS], mate_q.at[l, 0])
+        load(0)[2].start()
+        before = ({1: 2}, {0: 1, 1: 2})[l]
+        after = ({0: 1, 2: 3}, {2: 3})[l]
+
+        @pl.loop(0, NB)
+        def _(i):
+            p, slot, cp = load(i)
+            cp.wait()
+            for at, nxt in before.items():
+                @pl.when(i == at)
+                def _():
+                    fetch(nxt)
+            if l == 1:
+                @pl.when(i == 2)
+                def _():
+                    forward_far('q', O_SEQ)
+            qkv_step(p, slot)
+            for at, nxt in after.items():
+                @pl.when(i == at)
+                def _():
+                    fetch(nxt)
         tick((O_SEQ, PER + F_SEQ + 3)[l])
 
     lane = lax.broadcasted_iota(jnp.int32, (1, LANES), 1)

time: 560 us -> 551 us (0.984); the launches traced: 551 us -> 550 us
  no operation moved by 1% of the time
where the time goes in v3:
time: 551 us; the launch traced here: 550 us
  Pallas kernels  545 us (99%)
  local copies, waits for them, and re-layouts  5.89 us (1%)
    pallas_call x1, Pallas kernels, local_fn(): pl.pallas_call(mega_kernel, in_specs=[hbm, vmem, pl.BlockSpec(memory_spac...  545 us

profile of v3, /device:TPU:0, one launch (start us, length us, event | category | flops | bytes accessed | tf_op | source)
XLA Modules:
  0.0 550.4 jit_solution(16512858783524004478)
XLA Ops:
  0.0 544.5 %shard_map.118 = (bf16[8,256,1536]{2,1,0:T(8,128)(2,1)}, bf16[2,3072,1536]{2,1,0:T(8,128)(2,1)}, bf16[2,1024,1536]{2,1,0:T(8,128)(2,1)}, bf16[30,768,1536]{2,1,0:T(8,128)(2,1)}, bf16[2048,1536]{1,0:T(8,128)(2,1)}) custom-call(bf16[8,256,1536]{2,1,0:T(8,128)(2,1)} %tok.1, s32[8,2048]{1,0:T(8,128)} %pad.1, f32[2,32]{1,0:T(2,128)} %bitcast.5, ...), custom_call_target="tpu_custom_call" | custom-call | tf_op jit(solution)/shard_map/pallas_call | solution.py:662
  544.5 5.9 %copy.14 = bf16[8,256,1536]{2,1,0:T(8,128)(2,1)} copy(bf16[8,256,1536]{2,1,0:T(8,128)(2,1)} %get-tuple-element.6) | data formatting | bytes 12582912

commit v4 on v3

--- a/solution.py
+++ b/solution.py
@@ -28,6 +28,8 @@
 NF = 3 * NG
 LEAD = 5
 LAG = 5
+SWAP = 48
+KEEP = PART - SWAP
 VMEM_BYTES = 67043328
 
 SEQUENCE = []
@@ -72,9 +74,9 @@
 
 def mega_kernel(tok, pad, rel, wq, wk, wv, wo, wa, wl, wd, n1, n2,
                 out, gq, go, gf, xs,
-                X, U, B, W, wb, wo2, F, Fo, ka_ref, qa_ref, mx, rawq,
+                X, U, B, W, wb, wo2, away, here, Hx, Ux, F, Fo, ka_ref, qa_ref, mx, rawq,
                 near_q, near_o, near_f, far_q, far_o, far_f, mate_q, mate_o, mate_f, sent_q, sent_o, sent_f,
-                ts, tr, fts, ftr, ys, yr, ls, gs, vs, ps, rl):
+                ts, tr, fts, ftr, ys, yr, ss, sr, ls, gs, vs, ps, rl):
     me = lax.axis_index('tp')
     core, chip = me % 2, me // 2
     cx, cy = chip % 2, chip // 2
@@ -474,19 +476,24 @@
     def group_in(l, g):
         drained(gf.at[:3, :4 * FR], mate_f.at[NG * l + g])
 
-    def gated(slot, devs):
-        hm = jnp.concatenate([X[span(d * PART, PART), :] for d in devs])
+    def gated(slot, parts):
+        hm = jnp.concatenate([h[r, :] for h, _, r in parts])
         a = lax.dot_general(hm, B[slot, :GF, :], NT, preferred_element_type=F32)
         b = lax.dot_general(hm, B[slot, GF:2 * GF, :], NT, preferred_element_type=F32)
         return (gelu(a) * b).astype(BF16)
 
-    def add_down(slot, devs, g):
+    def add_down(slot, parts, g):
         y = jnp.dot(g, wb[slot], preferred_element_type=F32)
-        for i, d in enumerate(devs):
-            U[span(d * PART, PART), :] += y[i * PART:(i + 1) * PART]
-
-    def ffn_step(slot, devs):
-        add_down(slot, devs, gated(slot, devs))
+        at = 0
+        for _, total, r in parts:
+            total[r, :] += y[at:at + r.size]
+            at += r.size
+
+    def ffn_step(slot, parts):
+        add_down(slot, parts, gated(slot, parts))
+
+    def rows_of(devs, size=PART):
+        return [(X, U, span(d * PART, size)) for d in devs]
 
     def pair_of(m):
         return 2 * m, 2 * m + 1
@@ -502,17 +509,17 @@
     far_pair = pair_of(nd // 2)
 
     def near_pair(mi):
-        mine = mi // 3
-        return [(1 - mine) * (2 * (near // 2) + mi - 1) + mine * (2 * chip + i) for i, near in enumerate((nx, ny))]
-
-    def home(d):
-        return remote(X.at[pl.ds(d * PART, PART)], out.at[me], ys.at[0], yr.at[0], d)
-
-    def deliver(devs):
+        return [2 * (near // 2) + mi - 1 for near in (nx, ny)]
+
+    def home(d, rows=PART):
+        i = rows // PART
+        return remote(X.at[pl.ds(d * PART, rows)], out.at[me, :rows], ys.at[i], yr.at[i], d)
+
+    def deliver(devs, rows=PART):
         for d in devs:
-            r = span(d * PART, PART)
+            r = span(d * PART, rows)
             X[r, :] = U[r, :].astype(BF16)
-        start(home(d) for d in devs)
+        start(home(d, rows) for d in devs)
 
     seen = [(me, own_tok)] + [(peers[i], tcp[i]) for i in reversed(range(NDEV - 1))]
     back = [local(xs, X, vs.at[NDEV])]
@@ -545,6 +552,10 @@
         start(first)
         out_proj(gain2)
         tick((NF, NSEQ - 1)[l])
+        if l == 1:
+            for i, d in enumerate(far_pair):
+                away[i] = U[span(d * PART + KEEP, SWAP, HD // 4), :].astype(BF16)
+                remote(away.at[i], here.at[core], ss.at[0], sr.at[0], d).start()
         norm_block(NB - 1, gain2)
 
         if l == 0:
@@ -572,7 +583,7 @@
                 def _():
                     group_in(l, g + 1)
                     start(load_group(l, g + 1, g % 2))
-                ffn_step((g + 1) % 2, pair_of(m))
+                ffn_step((g + 1) % 2, rows_of(pair_of(m)))
             tick(22)
 
             @pl.loop(1, NB)
@@ -580,7 +591,7 @@
                 @pl.when(m > 2)
                 def _():
                     kept(m - 3).wait()
-                ffn_step(1, pair_of(m))
+                ffn_step(1, rows_of(pair_of(m)))
                 norm_block(m - 1, n1[1:, :], True)
                 kept(m - 1).start()
             kept(1).wait()
@@ -590,6 +601,7 @@
             continue
 
         tail = load_group(l, NG - 1, 1)
+        far_rows = rows_of(far_pair, KEEP)
 
         @pl.loop(0, NG - 1)
         def _(s):
@@ -610,43 +622,66 @@
             def _():
                 drained(gf.at[:2, :4 * FR], mate_f.at[LAYERS * NG - 1])
                 start(tail[:2])
-            ffn_step(slot, far_pair)
+            ffn_step(slot, far_rows)
 
         forward_far('f', LATE[-1])
         start(load_group(l, 0, 0))
         drained(gf.at[:2], gs.at[1])
-        g = gated(1, far_pair)
+        g = gated(1, far_rows)
         drained(gf.at[0, :4 * FR], mate_f.at[LAYERS * NG])
         tail[2].start()
         tail[2].wait()
-        add_down(1, far_pair, g)
-        deliver(far_pair)
+        add_down(1, far_rows, g)
+        deliver(far_pair, KEEP)
         all_sent(l)
 
-        @pl.loop(NG, NB * NG)
-        def _(s):
-            mi, g, slot = s // NG, s % NG, (s + 1) % 2
+        def last_steps(s, body):
+            g, slot = s % NG, (s + 1) % 2
             loaded(slot)
 
             @pl.when(s < NB * NG - 1)
             def _():
                 start(load_group(l, (g + 1) % NG, 1 - slot))
-            ffn_step(slot, near_pair(mi))
-
-            @pl.when(jnp.logical_and(g == NG - 1, mi < NB - 1))
+            body(slot)
+
+        @pl.loop(NG, 3 * NG)
+        def _(s):
+            devs = near_pair(s // NG)
+            last_steps(s, lambda slot: ffn_step(slot, rows_of(devs)))
+
+            @pl.when(s % NG == NG - 1)
             def _():
-                deliver(near_pair(mi))
+                deliver(devs)
+
+        drained(here, sr.at[0])
+        for i in range(2):
+            r = pl.ds(i * SWAP, SWAP)
+            v = here[i].astype(F32)
+            inv = lax.rsqrt(jnp.mean(v * v, axis=-1, keepdims=True) + 1e-6)
+            Hx[r, :] = (v * inv * gain2).astype(BF16)
+            Ux[r, :] = v
+        own_rows = rows_of(pair_of(chip)) + [(Hx, Ux, pl.ds(0, 2 * SWAP))]
+
+        @pl.loop(3 * NG, NB * NG)
+        def _(s):
+            last_steps(s, lambda slot: ffn_step(slot, own_rows))
 
     for d in (mate, me):
         r = span(d * PART, PART)
         X[r, :] = U[r, :].astype(BF16)
+    Hx[:, :] = Ux[:, :].astype(BF16)
     to_mate = home(mate)
     to_self = local(X.at[pl.ds(me * PART, PART)], out.at[me], vs.at[NDEV])
+    swapped = [local(Hx.at[pl.ds(i * SWAP, SWAP)], out.at[d, KEEP:], vs.at[i]) for i, d in enumerate(far_pair)]
+    start(swapped)
     start((to_mate, to_self))
     drained(tok.at[:NDEV - 1], ts.at[0])
-    drained(out.at[:NDEV - 1], ys.at[0])
-    drained(out.at[:NDEV - 1], yr.at[0])
+    drained(away, ss.at[0])
+    for sems in (ys, yr):
+        drained(out.at[:2, :KEEP], sems.at[0])
+        drained(out.at[:NDEV - 3], sems.at[1])
     to_self.wait()
+    wait(swapped)
 
 
 def solution(mesh):
@@ -666,12 +701,13 @@
             out_shape=[jax.ShapeDtypeStruct(s, BF16) for s in shapes],
             scratch_shapes=[
                 pltpu.VMEM((SEQ, DM), BF16), pltpu.VMEM((SEQ, DM), F32), pltpu.VMEM((2, SEQ, DM), BF16),
-                pltpu.VMEM((NH, 3, KC, KC), F32), pltpu.VMEM((2, GF, DM), BF16), pltpu.VMEM((KC, DM), BF16), pltpu.VMEM((NDEV, NDEV, 4 * KC), F32),
+                pltpu.VMEM((NH, 3, KC, KC), F32), pltpu.VMEM((2, GF, DM), BF16), pltpu.VMEM((KC, DM), BF16), pltpu.VMEM((2, SWAP, DM), BF16),
+                pltpu.VMEM((2, SWAP, DM), BF16), pltpu.VMEM((2 * SWAP, DM), BF16), pltpu.VMEM((2 * SWAP, DM), F32), pltpu.VMEM((NDEV, NDEV, 4 * KC), F32),
                 pltpu.VMEM((NDEV, 4 * KC), F32), pltpu.VMEM((LANES, SEQ), BF16), pltpu.VMEM((NH, NT_K, LANES), F32),
                 pltpu.VMEM((2, BQ, LANES), F32), pltpu.VMEM((LAYERS, 3, DM, LANES), BF16),
             ] + [sem((n, 2)) for n in chunks] + [sem((LAYERS,)), sem((LAYERS,)), sem((LAYERS * NF,))] + [
                 sem((LAYERS, 4)), sem((LAYERS,)), sem((LAYERS * NG + 1,)), sem((LAYERS,)), sem((LAYERS,)), sem((LAYERS * NG,)),
-                sem((1,)), sem((NDEV,))] + [sem((1,))] * 4 + [
+                sem((1,)), sem((NDEV,))] + [sem((1,))] * 2 + [sem((2,))] * 2 + [sem((1,))] * 2 + [
                 sem((2,)), sem((2,)), sem((NDEV + 1,)), sem((LAYERS, 2)), sem((LAYERS, 2))],
             compiler_params=pltpu.CompilerParams(collective_id=0, has_side_effects=True, vmem_limit_bytes=VMEM_BYTES),
         )(tokens, pad_mask, rel_table.T, w_query, w_key, w_value, w_out, jnp.swapaxes(w_act, 1, 2), jnp.swapaxes(w_lin, 1, 2),

time: 551 us -> 546 us (level)
  Pallas kernels: 545 us -> 539 us
where the time goes in v4:
time: 546 us; the launch traced here: 545 us
  Pallas kernels  539 us (99%)
  local copies, waits for them, and re-layouts  5.89 us (1%)
    pallas_call x1, Pallas kernels, local_fn(): pl.pallas_call(mega_kernel, in_specs=[hbm, vmem, pl.BlockSpec(memory_spac...  539 us

profile of v4, /device:TPU:0, one launch (start us, length us, event | category | flops | bytes accessed | tf_op | source)
XLA Modules:
  0.0 545.3 jit_solution(8205080906339823043)
XLA Ops:
  0.0 539.4 %shard_map.118 = (bf16[8,256,1536]{2,1,0:T(8,128)(2,1)}, bf16[2,3072,1536]{2,1,0:T(8,128)(2,1)}, bf16[2,1024,1536]{2,1,0:T(8,128)(2,1)}, bf16[30,768,1536]{2,1,0:T(8,128)(2,1)}, bf16[2048,1536]{1,0:T(8,128)(2,1)}) custom-call(bf16[8,256,1536]{2,1,0:T(8,128)(2,1)} %tok.1, s32[8,2048]{1,0:T(8,128)} %pad.1, f32[2,32]{1,0:T(2,128)} %bitcast.5, ...), custom_call_target="tpu_custom_call" | custom-call | tf_op jit(solution)/shard_map/pallas_call | solution.py:697
  539.4 5.9 %copy.14 = bf16[8,256,1536]{2,1,0:T(8,128)(2,1)} copy(bf16[8,256,1536]{2,1,0:T(8,128)(2,1)} %get-tuple-element.6) | data formatting | bytes 12582912

commit v5 on v4

--- a/solution.py
+++ b/solution.py
@@ -224,10 +224,10 @@
         start(stores[l][1:])
 
     m3 = split3(jnp.where(pad[pl.ds(me, 1), :] == 1, 0.0, -1e9).astype(F32) * LOG2E)
-    rowi = lax.broadcasted_iota(jnp.int32, (LANES, 1), 0) % HD
+    rowi = lax.broadcasted_iota(jnp.int32, (HD, 1), 0)
     for c in range(NT_K):
         col = slice(c * KC, (c + 1) * KC)
-        v = jnp.where(jnp.logical_and(rowi >= 3 * c, rowi < 3 * c + 3), 1.0, jnp.zeros((LANES, KC), F32))
+        v = jnp.where(jnp.logical_and(rowi >= 3 * c, rowi < 3 * c + 3), 1.0, jnp.zeros((HD, KC), F32))
         for p in range(3):
             v = jnp.where(rowi == 3 * NT_K + p, m3[p][:, col], v)
         ka_ref[:, col] = v.astype(BF16)
@@ -273,9 +273,9 @@
     def v_cols(pair):
         return span(1024 * (1 - pair // 4) + LANES * (pair % 4), LANES)
 
-    def k_at(pair, key, size):
+    def k_at(i, key, size, rows=LANES):
         half = SEQ // 2
-        return span((key // half) * half + pair * LANES, LANES), span(BQ + key % half, size)
+        return span((key // half) * half + i * rows, rows, rows), span(BQ + key % half, size)
 
     def qkv_step(p, slot):
         @pl.loop(0, NB)
@@ -333,7 +333,6 @@
         tick((O_SEQ, PER + F_SEQ + 3)[l])
 
     lane = lax.broadcasted_iota(jnp.int32, (1, LANES), 1)
-    krow = lax.broadcasted_iota(jnp.int32, (LANES, 1), 0)
     NU = NH * NB
     ones = jnp.ones((KC, LANES), BF16)
 
@@ -352,19 +351,18 @@
     def q_operand(u):
         h, i, pair, odd = parts(u)
         q32 = B[0, span(i * BQ, BQ), q_cols(pair)].astype(F32) * LOG2E
-        hi = q32.astype(BF16).astype(F32)
-        mine = (lane // HD) == odd
+        q32 = jnp.where((lane // HD) == odd, q32, pltpu.roll(q32, HD, 1))
+        hi, mid, low = split3(q32)
         qa = jnp.concatenate([jnp.broadcast_to(qa_ref[h, pl.ds(i * NSUB + r, 1), :], (KC, LANES)) for r in range(NSUB)])
-        return jnp.concatenate([jnp.where(mine, hi, 0.0).astype(BF16), jnp.where(mine, q32 - hi, qa).astype(BF16)], axis=1)
+        both = jnp.where(lane < HD, hi, low), jnp.where(lane < HD, mid, qa)
+        return jnp.concatenate([v.astype(BF16) for v in both], axis=1)
 
     def score_tile(u, qv, t, slot, m):
         h, i, pair, odd = parts(u)
         c = tile_at(i, t)
-        kr, kc = k_at(pair, c * KC, KC)
-        kp = B[1, kr, kc]
-        kx = ka_ref[:, span(c * KC, KC)]
-        sel = jnp.where((krow // HD) == odd, kp.astype(F32), kx.astype(F32)).astype(BF16)
-        s = jnp.dot(qv, jnp.concatenate([kp, sel]), preferred_element_type=F32)
+        kr, kc = k_at(h, c * KC, KC, HD)
+        kh = B[1, kr, kc]
+        s = jnp.dot(qv, jnp.concatenate([kh, kh, kh, ka_ref[:, span(c * KC, KC)]]), preferred_element_type=F32)
         r0, c0 = sblock(slot, t)
         ms = []
         for r in range(NSUB):
@@ -703,7 +701,7 @@
                 pltpu.VMEM((SEQ, DM), BF16), pltpu.VMEM((SEQ, DM), F32), pltpu.VMEM((2, SEQ, DM), BF16),
                 pltpu.VMEM((NH, 3, KC, KC), F32), pltpu.VMEM((2, GF, DM), BF16), pltpu.VMEM((KC, DM), BF16), pltpu.VMEM((2, SWAP, DM), BF16),
                 pltpu.VMEM((2, SWAP, DM), BF16), pltpu.VMEM((2 * SWAP, DM), BF16), pltpu.VMEM((2 * SWAP, DM), F32), pltpu.VMEM((NDEV, NDEV, 4 * KC), F32),
-                pltpu.VMEM((NDEV, 4 * KC), F32), pltpu.VMEM((LANES, SEQ), BF16), pltpu.VMEM((NH, NT_K, LANES), F32),
+                pltpu.VMEM((NDEV, 4 * KC), F32), pltpu.VMEM((HD, SEQ), BF16), pltpu.VMEM((NH, NT_K, LANES), F32),
                 pltpu.VMEM((2, BQ, LANES), F32), pltpu.VMEM((LAYERS, 3, DM, LANES), BF16),
             ] + [sem((n, 2)) for n in chunks] + [sem((LAYERS,)), sem((LAYERS,)), sem((LAYERS * NF,))] + [
                 sem((LAYERS, 4)), sem((LAYERS,)), sem((LAYERS * NG + 1,)), sem((LAYERS,)), sem((LAYERS,)), sem((LAYERS * NG,)),

time: 546 us -> 546 us (level)
  no operation moved by 1% of the time
where the time goes in v5:
time: 546 us; the launch traced here: 545 us
  Pallas kernels  539 us (99%)
  local copies, waits for them, and re-layouts  5.89 us (1%)
    pallas_call x1, Pallas kernels, local_fn(): pl.pallas_call(mega_kernel, in_specs=[hbm, vmem, pl.BlockSpec(memory_spac...  539 us

profile of v5, /device:TPU:0, one launch (start us, length us, event | category | flops | bytes accessed | tf_op | source)
XLA Modules:
  0.0 545.3 jit_solution(7257824669485170549)
XLA Ops:
  0.0 539.4 %shard_map.118 = (bf16[8,256,1536]{2,1,0:T(8,128)(2,1)}, bf16[2,3072,1536]{2,1,0:T(8,128)(2,1)}, bf16[2,1024,1536]{2,1,0:T(8,128)(2,1)}, bf16[30,768,1536]{2,1,0:T(8,128)(2,1)}, bf16[2048,1536]{1,0:T(8,128)(2,1)}) custom-call(bf16[8,256,1536]{2,1,0:T(8,128)(2,1)} %tok.1, s32[8,2048]{1,0:T(8,128)} %pad.1, f32[2,32]{1,0:T(2,128)} %bitcast.5, ...), custom_call_target="tpu_custom_call" | custom-call | tf_op jit(solution)/shard_map/pallas_call | solution.py:695
  539.4 5.9 %copy.14 = bf16[8,256,1536]{2,1,0:T(8,128)(2,1)} copy(bf16[8,256,1536]{2,1,0:T(8,128)(2,1)} %get-tuple-element.6) | data formatting | bytes 12582912

commit v6 on v5

--- a/solution.py
+++ b/solution.py
@@ -26,9 +26,10 @@
 NG = SHARD // FR
 GF = NDEV * FR
 NF = 3 * NG
+POOL = NF - NG
 LEAD = 5
 LAG = 5
-SWAP = 48
+SWAP = 32
 KEEP = PART - SWAP
 VMEM_BYTES = 67043328
 
@@ -72,9 +73,9 @@
         c.wait()
 
 
-def mega_kernel(tok, pad, rel, wq, wk, wv, wo, wa, wl, wd, n1, n2,
+def mega_kernel(tok, pad_in, rel_in, wq, wk, wv, wo, wa, wl, wd, n1_in, n2_in,
                 out, gq, go, gf, xs,
-                X, U, B, W, wb, wo2, away, here, Hx, Ux, F, Fo, ka_ref, qa_ref, mx, rawq,
+                X, U, B, W, wb, wo2, away, here, Hx, Ux, F, Fo, ka_ref, qa_ref, mx, rawq, pad, rel, n1, n2,
                 near_q, near_o, near_f, far_q, far_o, far_f, mate_q, mate_o, mate_f, sent_q, sent_o, sent_f,
                 ts, tr, fts, ftr, ys, yr, ss, sr, ls, gs, vs, ps, rl):
     me = lax.axis_index('tp')
@@ -113,9 +114,9 @@
         near, far, via, sent = {'q': (near_q, far_q, mate_q, sent_q), 'o': (near_o, far_o, mate_o, sent_o),
                                 'f': (near_f, far_f, mate_f, sent_f)}[kind]
         if slot < 2:
-            got = near.at[k, slot]
+            got = near.at[k % POOL if kind == 'f' else k, slot]
         elif slot in (3, 4):
-            got = far.at[k // 3 if kind == 'q' else k]
+            got = far.at[k // 3 if kind == 'q' else k % NF]
         elif kind == 'q':
             got = via.at[k // 3, max(slot - 4, 0)]
         else:
@@ -135,7 +136,7 @@
             drained(gq.at[k // 3, :QROWS], far_q.at[k // 3])
             start(hop(kind, k + i, EVERY[-1]) for i in range(3))
         else:
-            drained(place(kind, k, 0, 0, ROWS[kind]), (far_o if kind == 'o' else far_f).at[k])
+            drained(place(kind, k, 0, 0, ROWS[kind]), (far_o if kind == 'o' else far_f).at[k % NF])
             hop(kind, k, EVERY[-1]).start()
 
     def tick(s):
@@ -182,6 +183,8 @@
     barrier = pltpu.get_barrier_semaphore()
     for o in EVERY[1:]:
         pl.semaphore_signal(barrier, inc=1, device_id={'tp': (me + o) % NDEV}, device_id_type=MESH)
+    small = [local(a, b, vs.at[i]) for i, (a, b) in enumerate(((rel_in, rel), (pad_in, pad), (n1_in, n1), (n2_in, n2)))]
+    start(small)
     stores = [store_own(l) for l in range(LAYERS)]
     for l in range(LAYERS):
         start(load_raw(l))
@@ -192,6 +195,8 @@
     tcp = [remote(tok.at[d], X.at[pl.ds(me * PART, PART)], ts.at[0], tr.at[i], d) for i, d in enumerate(peers)]
     own_tok = local(tok.at[me], X.at[pl.ds(me * PART, PART)], vs.at[NDEV])
     start((*tcp[2:], own_tok))
+    wait(small)
+    table = rel[:, :] * LOG2E
 
     t = lax.broadcasted_iota(jnp.int32, (1, 4 * KC), 1)
     n = jnp.where(t < 3 * KC, t, t - 4 * KC) - KC
@@ -201,7 +206,7 @@
     for h in range(2):
         row = jnp.zeros((1, 4 * KC), F32)
         for b in range(32):
-            row = jnp.where(bucket == b, rel[h, b] * LOG2E, row)
+            row = jnp.where(bucket == b, table[h:h + 1, b:b + 1], row)
         Fo[pl.ds(h, 1), :] = row
     Fo[2:, :] = jnp.zeros((NDEV - 2, 4 * KC), F32)
 
@@ -688,13 +693,12 @@
 
     def local_fn(tokens, pad_mask, rel_table, w_query, w_key, w_value, w_out, w_act, w_lin, w_down, norm_attn, norm_mlp):
         hbm = pl.BlockSpec(memory_space=pltpu.MemorySpace.HBM)
-        vmem = pl.BlockSpec(memory_space=pltpu.VMEM)
         sem = pltpu.SemaphoreType.DMA
         shapes = [(NDEV, PART, DM), (LAYERS, NDEV * QROWS, DM), (LAYERS, NDEV * HROWS, DM), (LAYERS * NF, GF, DM), (SEQ, DM)]
-        chunks = (O_SEQ * LAYERS, LAYERS, LAYERS * NF)
+        chunks = (O_SEQ * LAYERS, LAYERS, POOL)
         return pl.pallas_call(
             mega_kernel,
-            in_specs=[hbm, vmem, pl.BlockSpec(memory_space=pltpu.SMEM)] + [hbm] * 7 + [vmem] * 2,
+            in_specs=[hbm] * 12,
             out_specs=[hbm] * 5,
             out_shape=[jax.ShapeDtypeStruct(s, BF16) for s in shapes],
             scratch_shapes=[
@@ -703,7 +707,8 @@
                 pltpu.VMEM((2, SWAP, DM), BF16), pltpu.VMEM((2 * SWAP, DM), BF16), pltpu.VMEM((2 * SWAP, DM), F32), pltpu.VMEM((NDEV, NDEV, 4 * KC), F32),
                 pltpu.VMEM((NDEV, 4 * KC), F32), pltpu.VMEM((HD, SEQ), BF16), pltpu.VMEM((NH, NT_K, LANES), F32),
                 pltpu.VMEM((2, BQ, LANES), F32), pltpu.VMEM((LAYERS, 3, DM, LANES), BF16),
-            ] + [sem((n, 2)) for n in chunks] + [sem((LAYERS,)), sem((LAYERS,)), sem((LAYERS * NF,))] + [
+                pltpu.VMEM((NDEV, SEQ), jnp.int32), pltpu.VMEM((2, 32), F32), pltpu.VMEM((LAYERS, DM), F32), pltpu.VMEM((LAYERS, DM), F32),
+            ] + [sem((n, 2)) for n in chunks] + [sem((LAYERS,)), sem((LAYERS,)), sem((NF,))] + [
                 sem((LAYERS, 4)), sem((LAYERS,)), sem((LAYERS * NG + 1,)), sem((LAYERS,)), sem((LAYERS,)), sem((LAYERS * NG,)),
                 sem((1,)), sem((NDEV,))] + [sem((1,))] * 2 + [sem((2,))] * 2 + [sem((1,))] * 2 + [
                 sem((2,)), sem((2,)), sem((NDEV + 1,)), sem((LAYERS, 2)), sem((LAYERS, 2))],

time: 546 us -> 544 us (level)
  no operation moved by 1% of the time
where the time goes in v6:
time: 544 us; the launch traced here: 543 us
  Pallas kernels  537 us (99%)
  local copies, waits for them, and re-layouts  5.89 us (1%)
    pallas_call x1, Pallas kernels, local_fn(): pl.pallas_call(mega_kernel, in_specs=[hbm] * 12, out_specs=[hbm] * 5, out...  537 us

profile of v6, /device:TPU:0, one launch (start us, length us, event | category | flops | bytes accessed | tf_op | source)
XLA Modules:
  0.0 543.4 jit_solution(8933926032548309934)
XLA Ops:
  0.0 537.5 %shard_map.118 = (bf16[8,256,1536]{2,1,0:T(8,128)(2,1)}, bf16[2,3072,1536]{2,1,0:T(8,128)(2,1)}, bf16[2,1024,1536]{2,1,0:T(8,128)(2,1)}, bf16[30,768,1536]{2,1,0:T(8,128)(2,1)}, bf16[2048,1536]{1,0:T(8,128)(2,1)}) custom-call(bf16[8,256,1536]{2,1,0:T(8,128)(2,1)} %tok.1, s32[8,2048]{1,0:T(8,128)} %pad_in.1, f32[2,32]{1,0:T(2,128)} %bitcast.5, ...), custom_call_target="tpu_custom_call" | custom-call | tf_op jit(solution)/shard_map/pallas_call | solution.py:699
  537.5 5.9 %copy.14 = bf16[8,256,1536]{2,1,0:T(8,128)(2,1)} copy(bf16[8,256,1536]{2,1,0:T(8,128)(2,1)} %get-tuple-element.6) | data formatting | bytes 12582912

commit v7 on v6

--- a/solution.py
+++ b/solution.py
@@ -29,7 +29,7 @@
 POOL = NF - NG
 LEAD = 5
 LAG = 5
-SWAP = 32
+SWAP = 16
 KEEP = PART - SWAP
 VMEM_BYTES = 67043328
 

time: 544 us -> 557 us (1.024); the launches traced: 543 us -> 550 us
  Pallas kernels: 537 us -> 543 us
    pallas_call x1, Pallas kernels: 537 us -> 543 us  [local_fn(): pl.pallas_call(mega_kernel, in_specs=[hbm] * 12, out_specs=[hbm] * 5, out...]
where the time goes in v7:
time: 557 us; the launch traced here: 550 us
  Pallas kernels  543 us (97%)
  local copies, waits for them, and re-layouts  5.89 us (1%)
    pallas_call x1, Pallas kernels, local_fn(): pl.pallas_call(mega_kernel, in_specs=[hbm] * 12, out_specs=[hbm] * 5, out...  543 us

profile of v7, /device:TPU:0, one launch (start us, length us, event | category | flops | bytes accessed | tf_op | source)
XLA Modules:
  0.0 549.6 jit_solution(17016154026697902242)
XLA Ops:
  0.0 543.3 %shard_map.118 = (bf16[8,256,1536]{2,1,0:T(8,128)(2,1)}, bf16[2,3072,1536]{2,1,0:T(8,128)(2,1)}, bf16[2,1024,1536]{2,1,0:T(8,128)(2,1)}, bf16[30,768,1536]{2,1,0:T(8,128)(2,1)}, bf16[2048,1536]{1,0:T(8,128)(2,1)}) custom-call(bf16[8,256,1536]{2,1,0:T(8,128)(2,1)} %tok.1, s32[8,2048]{1,0:T(8,128)} %pad_in.1, f32[2,32]{1,0:T(2,128)} %bitcast.5, ...), custom_call_target="tpu_custom_call" | custom-call | tf_op jit(solution)/shard_map/pallas_call | solution.py:699
  543.3 5.9 %copy.14 = bf16[8,256,1536]{2,1,0:T(8,128)(2,1)} copy(bf16[8,256,1536]{2,1,0:T(8,128)(2,1)} %get-tuple-element.6) | data formatting | bytes 12582912
